TPU v7x, 32 devices: a whole 2x2x4 slice. The times are simulated.
32 devices in a mesh: dp: 2 (over x), tp: 16 (over y, z, core).
Axes of the slice: x: 2, y: 2, z: 4, core: 2. Of those that a mesh axis runs over, the one named last changes fastest.
Arguments:
- x: bfloat16 [11264, 3072], P(('dp', 'tp')), parts along dimension 0
- dy: bfloat16 [11264, 3072], P(('dp', 'tp')), parts along dimension 0
- gate: bfloat16 [11264, 24576], P('dp', 'tp'), parts along dimension 0
- up: bfloat16 [11264, 24576], P('dp', 'tp'), parts along dimension 0
- w_gate: bfloat16 [3072, 24576], P(None, 'tp')
- w_up: bfloat16 [3072, 24576], P(None, 'tp')
- w_down: bfloat16 [24576, 3072], P('tp')
Outputs:
- output 1: bfloat16 [11264, 3072], P(('dp', 'tp')), parts along dimension 0
- output 2: bfloat16 [6144, 24576], P('dp', 'tp'), parts along dimension 0
- output 3: bfloat16 [6144, 24576], P('dp', 'tp'), parts along dimension 0
- output 4: bfloat16 [49152, 3072], P(('dp', 'tp')), parts along dimension 0
There are 2 independent parts. A program takes and returns all parts, laid end to end along the dimension named above; an argument that names none is the same for every part.
All inputs are finite; a program needn't handle non-finite values.
Results may differ from a plain program's by a relative error of at most 0.012.
Values are sent between devices in bfloat16 or wider.
A program may use at most 2 GiB of HBM per device.

v0:
```python
import jax
import jax.numpy as jnp


def act(gate, up):
    return jax.nn.gelu(gate) * up


def solution(mesh):
    def step(x, dy, gate, up, w_gate, w_up, w_down):
        hidden, back = jax.vjp(act, gate.astype(jnp.float32), up.astype(jnp.float32))
        d_hidden = jnp.dot(dy, w_down.T, preferred_element_type=jnp.float32)
        d_gate, d_up = (g.astype(jnp.bfloat16) for g in back(d_hidden))
        dx = jnp.dot(d_gate, w_gate.T) + jnp.dot(d_up, w_up.T)
        groups = mesh.shape["dp"]

        def by_group(a, b):
            a, b = (t.reshape(groups, -1, t.shape[-1]) for t in (a, b))
            product = jnp.einsum("gta,gtb->gab", a, b, preferred_element_type=jnp.float32)
            return product.astype(jnp.bfloat16).reshape(-1, b.shape[-1])

        return dx, by_group(x, d_gate), by_group(x, d_up), by_group(hidden.astype(jnp.bfloat16), dy)

    return step
```

profile of v0, /device:TPU:0, one launch (start us, length us, event | category | flops | bytes accessed | tf_op | source)
XLA Modules:
  0.0 1092.4 jit_solution(8965946703186332764)
XLA Ops:
  7.2 3.1 copy.15
  10.3 0.0 all-gather.11.cloned.1.call-start
  10.4 0.7 all-gather.11.cloned.1.call-update
  11.1 175.0 %all-gather.9.cloned.1.call-done = bf16[5632,3072]{1,0:T(8,128)(2,1)} async-done(((bf16[352,3072]{1,0:T(8,128)(2,1)}), bf16[5632,3072]{1,0:T(8,128)(2,1)}) %all-gather.9.cloned.1.call-update) | async-done | bytes 34603024 | tf_op args[1]
  186.1 63.6 %fusion.28 = f32[5632,1536]{1,0:T(8,128)} fusion(bf16[5632,3072]{1,0:T(8,128)(2,1)} %all-gather.9.cloned.1.call-done, bf16[1536,3072]{1,0:T(8,128)(2,1)} %param.3), kind=kOutput, calls=%fused_computation.46 | convolution fusion | flops 53150220288 | bytes 78643200 | tf_op jit(solution)/dot_general | solution.py:12
  249.7 36.4 %fusion.25 = (bf16[1,5632,1536]{2,1,0:T(8,128)(2,1)}, bf16[5632,1536]{1,0:T(8,128)(2,1)}) fusion(bf16[5632,1536]{1,0:T(8,128)(2,1)} %param.4, bf16[5632,1536]{1,0:T(8,128)(2,1)} %param.5, f32[5632,1536]{1,0:T(8,128)} %fusion.28), kind=kLoop, calls=%fused_computation.40 | loop fusion | flops 224919552 | bytes 103809024 | tf_op jit(solution)/reshape | solution.py:18
  286.1 61.7 %fusion.29 = bf16[5632,3072]{1,0:T(8,128)(2,1)} fusion(bf16[5632,1536]{1,0:T(8,128)(2,1)} %get-tuple-element.40, bf16[3072,1536]{1,0:T(8,128)(2,1)} %param.6), kind=kOutput, calls=%fused_computation.47 | convolution fusion | flops 53150220288 | bytes 61341696 | tf_op jit(solution)/dot_general | solution.py:14
  347.8 68.3 %convolution_add_fusion = bf16[5632,3072]{1,0:T(8,128)(2,1)} fusion(bf16[5632,3072]{1,0:T(8,128)(2,1)} %fusion.29, bf16[3072,1536]{1,0:T(8,128)(2,1)} %param.7, f32[5632,1536]{1,0:T(8,128)} %fusion.28, bf16[5632,1536]{1,0:T(8,128)(2,1)} %param.5), kind=kOutput, calls=%fused_computation.39 | convolution fusion | flops 53262680064 | bytes 130547712 | tf_op jit(solution)/dot_general | solution.py:14
  416.1 0.3 collective-permute-start.4
  416.4 74.8 %fusion.27 = bf16[3072,1536]{0,1:T(8,128)(2,1)} fusion(bf16[5632,3072]{1,0:T(8,128)(2,1)} %all-gather.11.cloned.1.call-done, f32[5632,1536]{1,0:T(8,128)} %fusion.28, bf16[5632,1536]{1,0:T(8,128)(2,1)} %param.5), kind=kOutput, calls=%fused_computation.44 | convolution fusion | flops 53250097152 | bytes 95944704 | tf_op jit(solution)/gta,gtb->gab/dot_general | solution.py:19
  491.2 64.2 %fusion.26 = bf16[3072,1536]{0,1:T(8,128)(2,1)} fusion(bf16[5632,1536]{1,0:T(8,128)(2,1)} %get-tuple-element.40, bf16[5632,3072]{1,0:T(8,128)(2,1)} %all-gather.11.cloned.1.call-done), kind=kOutput, calls=%fused_computation.43 | convolution fusion | flops 53154938880 | bytes 61341696 | tf_op jit(solution)/gta,gtb->gab/dot_general | solution.py:19
  555.4 12.6 %copy = bf16[3072,1536]{1,0:T(8,128)(2,1)} copy(bf16[3072,1536]{0,1:T(8,128)(2,1)} %fusion.26) | data formatting | bytes 18874368
  568.0 12.6 %copy.1 = bf16[3072,1536]{1,0:T(8,128)(2,1)} copy(bf16[3072,1536]{0,1:T(8,128)(2,1)} %fusion.27) | data formatting | bytes 18874368
  580.6 493.4 %while.2 = (bf16[1,5632,1536]{2,1,0:T(8,128)(2,1)}, bf16[1,1,352,3072]{3,2,1,0:T(8,128)(2,1)}, f32[1,1536,3072]{2,1,0:T(8,128)}, bf16[1,1,352,3072]{3,2,1,0:T(8,...) while((bf16[1,5632,1536]{2,1,0:T(8,128)(2,1)}, ...), condition=%wide.windowed_dot_general_cond_ag.clone, body=%wide.windowed_dot_general_body_ag.clone.sunk | while | flops 13314686976 | bytes 153354800 | solution.py:19
  580.9 4.2 collective-permute-start
  585.1 0.6 dynamic-slice.65
  587.6 13.6 %fusion.45 = f32[1536,3072,1]{1,0,2:T(8,128)} fusion(bf16[1,1,352,3072]{3,2,1,0:T(8,128)(2,1)} %get-tuple-element.86, bf16[1,1,352,3072]{3,2,1,0:T(8,128)(2,1)} %get-tuple-element.84, s32[]{:T(128)S(6)} %multiply.17, bf16[1,1,5632,1536]{3,2,1,0:T(8,128)(2,1)} %bitcast.67, s32[]{:T(128)S(6)} %multiply.18), kind=kOutput, calls=%fused_computation.7.clone.1 | convolution fusion | flops 6650265600 | bytes 40501256 | tf_op jit(solution)/gta,gtb->gab/dot_general | solution.py:19
  601.3 59.4 %collective-permute-done = bf16[1,1,352,3072]{3,2,1,0:T(8,128)(2,1)S(1)} collective-permute-done((bf16[1,1,352,3072]{3,2,1,0:T(8,128)(2,1)}, bf16[1,1,352,3072]{3,2,1,0:T(8,128)(2,1)S(1)}, u32[]{:S(2)}, u32[]{:S(2)}) %collective-permute-start) | collective-permute-done | bytes 2162720 | tf_op jit(solution)/gta,gtb->gab/dot_general | solution.py:19
  660.7 4.6 collective-permute-start.1
  665.3 0.3 collective-permute-done.2
  665.6 19.3 %bitcast_add_fusion.3 = f32[1,1536,3072]{2,1,0:T(8,128)} fusion(f32[1536,3072,1]{1,0,2:T(8,128)} %fusion.45, f32[1,1536,3072]{2,1,0:T(8,128)} %get-tuple-element.85, pred[]{:T(512)S(6)} %compare.6, bf16[1,1,352,3072]{3,2,1,0:T(8,128)(2,1)} %collective-permute-done.2, bf16[1,1,352,3072]{3,2,1,0:T(8,128)(2,1)S(1)} %collective-permute-done, ...), kind=kOutput, calls=%fused_computation.4.clone.1 | convolution fusion | flops 6664421376 | bytes 78249992 | tf_op jit(solution)/gta,gtb->gab/dot_general | solution.py:19
  684.9 24.5 %collective-permute-done.1 = bf16[1,1,352,3072]{3,2,1,0:T(8,128)(2,1)} collective-permute-done((bf16[1,1,352,3072]{3,2,1,0:T(8,128)(2,1)S(1)}, bf16[1,1,352,3072]{3,2,1,0:T(8,128)(2,1)}, u32[]{:S(2)}, u32[]{:S(2)}) %collective-permute-start.1) | collective-permute-done | bytes 2162720 | tf_op jit(solution)/gta,gtb->gab/dot_general | solution.py:19
  709.4 4.7 collective-permute-done.3
  714.2 0.5 collective-permute-start.2
  714.7 0.6 dynamic-slice.65
  717.2 13.6 %fusion.45 = f32[1536,3072,1]{1,0,2:T(8,128)} fusion(bf16[1,1,352,3072]{3,2,1,0:T(8,128)(2,1)} %get-tuple-element.86, bf16[1,1,352,3072]{3,2,1,0:T(8,128)(2,1)} %get-tuple-element.84, s32[]{:T(128)S(6)} %multiply.17, bf16[1,1,5632,1536]{3,2,1,0:T(8,128)(2,1)} %bitcast.67, s32[]{:T(128)S(6)} %multiply.18), kind=kOutput, calls=%fused_computation.7.clone.1 | convolution fusion | flops 6650265600 | bytes 40501256 | tf_op jit(solution)/gta,gtb->gab/dot_general | solution.py:19
  730.8 58.6 %collective-permute-done = bf16[1,1,352,3072]{3,2,1,0:T(8,128)(2,1)S(1)} collective-permute-done((bf16[1,1,352,3072]{3,2,1,0:T(8,128)(2,1)}, bf16[1,1,352,3072]{3,2,1,0:T(8,128)(2,1)S(1)}, u32[]{:S(2)}, u32[]{:S(2)}) %collective-permute-start) | collective-permute-done | bytes 2162720 | tf_op jit(solution)/gta,gtb->gab/dot_general | solution.py:19
  789.4 4.6 collective-permute-start.1
  794.1 0.8 collective-permute-start.3
  794.8 23.4 %bitcast_add_fusion.3 = f32[1,1536,3072]{2,1,0:T(8,128)} fusion(f32[1536,3072,1]{1,0,2:T(8,128)} %fusion.45, f32[1,1536,3072]{2,1,0:T(8,128)} %get-tuple-element.85, pred[]{:T(512)S(6)} %compare.6, bf16[1,1,352,3072]{3,2,1,0:T(8,128)(2,1)} %collective-permute-done.2, bf16[1,1,352,3072]{3,2,1,0:T(8,128)(2,1)S(1)} %collective-permute-done, ...), kind=kOutput, calls=%fused_computation.4.clone.1 | convolution fusion | flops 6664421376 | bytes 78249992 | tf_op jit(solution)/gta,gtb->gab/dot_general | solution.py:19
  818.3 58.4 %collective-permute-done.1 = bf16[1,1,352,3072]{3,2,1,0:T(8,128)(2,1)} collective-permute-done((bf16[1,1,352,3072]{3,2,1,0:T(8,128)(2,1)S(1)}, bf16[1,1,352,3072]{3,2,1,0:T(8,128)(2,1)}, u32[]{:S(2)}, u32[]{:S(2)}) %collective-permute-start.1) | collective-permute-done | bytes 2162720 | tf_op jit(solution)/gta,gtb->gab/dot_general | solution.py:19
  876.7 2.7 collective-permute-done.3
  879.4 1.9 collective-permute-start
  881.3 0.6 dynamic-slice.65
  883.8 13.6 %fusion.45 = f32[1536,3072,1]{1,0,2:T(8,128)} fusion(bf16[1,1,352,3072]{3,2,1,0:T(8,128)(2,1)} %get-tuple-element.86, bf16[1,1,352,3072]{3,2,1,0:T(8,128)(2,1)} %get-tuple-element.84, s32[]{:T(128)S(6)} %multiply.17, bf16[1,1,5632,1536]{3,2,1,0:T(8,128)(2,1)} %bitcast.67, s32[]{:T(128)S(6)} %multiply.18), kind=kOutput, calls=%fused_computation.7.clone.1 | convolution fusion | flops 6650265600 | bytes 40501256 | tf_op jit(solution)/gta,gtb->gab/dot_general | solution.py:19
  897.5 29.2 %collective-permute-done = bf16[1,1,352,3072]{3,2,1,0:T(8,128)(2,1)S(1)} collective-permute-done((bf16[1,1,352,3072]{3,2,1,0:T(8,128)(2,1)}, bf16[1,1,352,3072]{3,2,1,0:T(8,128)(2,1)S(1)}, u32[]{:S(2)}, u32[]{:S(2)}) %collective-permute-start) | collective-permute-done | bytes 2162720 | tf_op jit(solution)/gta,gtb->gab/dot_general | solution.py:19
  926.6 4.6 collective-permute-start.1
  931.2 23.5 %bitcast_add_fusion.3 = f32[1,1536,3072]{2,1,0:T(8,128)} fusion(f32[1536,3072,1]{1,0,2:T(8,128)} %fusion.45, f32[1,1536,3072]{2,1,0:T(8,128)} %get-tuple-element.85, pred[]{:T(512)S(6)} %compare.6, bf16[1,1,352,3072]{3,2,1,0:T(8,128)(2,1)} %collective-permute-done.2, bf16[1,1,352,3072]{3,2,1,0:T(8,128)(2,1)S(1)} %collective-permute-done, ...), kind=kOutput, calls=%fused_computation.4.clone.1 | convolution fusion | flops 6664421376 | bytes 78249992 | tf_op jit(solution)/gta,gtb->gab/dot_general | solution.py:19
  954.7 20.6 %collective-permute-done.1 = bf16[1,1,352,3072]{3,2,1,0:T(8,128)(2,1)} collective-permute-done((bf16[1,1,352,3072]{3,2,1,0:T(8,128)(2,1)S(1)}, bf16[1,1,352,3072]{3,2,1,0:T(8,128)(2,1)}, u32[]{:S(2)}, u32[]{:S(2)}) %collective-permute-start.1) | collective-permute-done | bytes 2162720 | tf_op jit(solution)/gta,gtb->gab/dot_general | solution.py:19
  975.3 1.1 collective-permute-done.3
  976.4 3.6 collective-permute-start
  980.0 0.6 dynamic-slice.65
  982.5 13.6 %fusion.45 = f32[1536,3072,1]{1,0,2:T(8,128)} fusion(bf16[1,1,352,3072]{3,2,1,0:T(8,128)(2,1)} %get-tuple-element.86, bf16[1,1,352,3072]{3,2,1,0:T(8,128)(2,1)} %get-tuple-element.84, s32[]{:T(128)S(6)} %multiply.17, bf16[1,1,5632,1536]{3,2,1,0:T(8,128)(2,1)} %bitcast.67, s32[]{:T(128)S(6)} %multiply.18), kind=kOutput, calls=%fused_computation.7.clone.1 | convolution fusion | flops 6650265600 | bytes 40501256 | tf_op jit(solution)/gta,gtb->gab/dot_general | solution.py:19
  996.2 28.9 %collective-permute-done = bf16[1,1,352,3072]{3,2,1,0:T(8,128)(2,1)S(1)} collective-permute-done((bf16[1,1,352,3072]{3,2,1,0:T(8,128)(2,1)}, bf16[1,1,352,3072]{3,2,1,0:T(8,128)(2,1)S(1)}, u32[]{:S(2)}, u32[]{:S(2)}) %collective-permute-start) | collective-permute-done | bytes 2162720 | tf_op jit(solution)/gta,gtb->gab/dot_general | solution.py:19
  1025.1 4.6 collective-permute-start.1
  1029.7 23.5 %bitcast_add_fusion.3 = f32[1,1536,3072]{2,1,0:T(8,128)} fusion(f32[1536,3072,1]{1,0,2:T(8,128)} %fusion.45, f32[1,1536,3072]{2,1,0:T(8,128)} %get-tuple-element.85, pred[]{:T(512)S(6)} %compare.6, bf16[1,1,352,3072]{3,2,1,0:T(8,128)(2,1)} %collective-permute-done.2, bf16[1,1,352,3072]{3,2,1,0:T(8,128)(2,1)S(1)} %collective-permute-done, ...), kind=kOutput, calls=%fused_computation.4.clone.1 | convolution fusion | flops 6664421376 | bytes 78249992 | tf_op jit(solution)/gta,gtb->gab/dot_general | solution.py:19
  1053.2 20.9 %collective-permute-done.1 = bf16[1,1,352,3072]{3,2,1,0:T(8,128)(2,1)} collective-permute-done((bf16[1,1,352,3072]{3,2,1,0:T(8,128)(2,1)S(1)}, bf16[1,1,352,3072]{3,2,1,0:T(8,128)(2,1)}, u32[]{:S(2)}, u32[]{:S(2)}) %collective-permute-start.1) | collective-permute-done | bytes 2162720 | tf_op jit(solution)/gta,gtb->gab/dot_general | solution.py:19
  1074.0 11.3 %convert_bitcast_fusion = bf16[1536,3072]{1,0:T(8,128)(2,1)} fusion(f32[1,1536,3072]{2,1,0:T(8,128)} %get-tuple-element.6), kind=kLoop, calls=%fused_computation.45 | loop fusion | flops 4718592 | bytes 28311552 | tf_op jit(solution)/reshape | solution.py:20
  (21 shorter events, 0.1 us)
Async XLA Ops:
  7.2 178.9 %all-gather.9.cloned.1.call-start = ((), (), s32[]{:S(2)}) async-start(), calls=%async_computation.1 | async-start | bytes 36765696 | tf_op args[1]
  10.3 406.1 %all-gather.11.cloned.1.call-start = ((), (), s32[]{:S(2)}) async-start(), calls=%async_computation.2 | async-start | bytes 36765696 | tf_op jit(solution)/reshape | solution.py:18
  11.1 1074.3 %reduce-scatter.4.cloned.1.call-start = ((), (), s32[]{:S(2)}) async-start(), calls=%async_computation.3 | async-start | bytes 36765696
  416.1 164.5 %collective-permute-start.4 = (bf16[1,1,352,3072]{3,2,1,0:T(8,128)(2,1)}, bf16[1,1,352,3072]{3,2,1,0:T(8,128)(2,1)}, u32[]{:S(2)}, u32[]{:S(2)}) collective-permute-start(bf16[1,1,352,3072]{3,2,1,0:T(8,128)(2,1)} %bitcast.8), channel_id=9, source_target_pairs={{0,1},{1,2},{2,3},{3,4},{4,5},{5,6},{6,7},{7,8},{8,9},{9,10},{10,1... | collective-permute-start | bytes 6488072 | tf_op jit(solution)/gta,gtb->gab/dot_general | solution.py:19
  555.4 25.2 %copy-start = (u32[32]{0:T(128)S(1)}, u32[32]{0:T(128)}, u32[]{:S(2)}) copy-start(u32[32]{0:T(128)} %constant.166) | copy-start | bytes 388
  580.9 79.8 %collective-permute-start = (bf16[1,1,352,3072]{3,2,1,0:T(8,128)(2,1)}, bf16[1,1,352,3072]{3,2,1,0:T(8,128)(2,1)S(1)}, u32[]{:S(2)}, u32[]{:S(2)}) collective-permute-start(bf16[1,1,352,3072]{3,2,1,0:T(8,128)(2,1)} %get-tuple-element.84), channel_id=10, source_target_pairs={{0,15},{1,0},{2,1},{3,2},{4,3},{5,4},{6,5},{7,6},{8,7},{9,8},{10,9... | collective-permute-start | bytes 6488072 | tf_op jit(solution)/gta,gtb->gab/dot_general | solution.py:19
  585.1 80.5 %collective-permute-start.2 = (bf16[1,1,352,3072]{3,2,1,0:T(8,128)(2,1)}, bf16[1,1,352,3072]{3,2,1,0:T(8,128)(2,1)}, u32[]{:S(2)}, u32[]{:S(2)}) collective-permute-start(bf16[1,1,352,3072]{3,2,1,0:T(8,128)(2,1)} %get-tuple-element.86), channel_id=11, source_target_pairs={{0,1},{1,2},{2,3},{3,4},{4,5},{5,6},{6,7},{7,8},{8,9},{9,10},{10,1... | collective-permute-start | bytes 6488072 | tf_op jit(solution)/gta,gtb->gab/dot_general | solution.py:19
  660.7 48.8 %collective-permute-start.1 = (bf16[1,1,352,3072]{3,2,1,0:T(8,128)(2,1)S(1)}, bf16[1,1,352,3072]{3,2,1,0:T(8,128)(2,1)}, u32[]{:S(2)}, u32[]{:S(2)}) collective-permute-start(bf16[1,1,352,3072]{3,2,1,0:T(8,128)(2,1)S(1)} %collective-permute-done), channel_id=12, source_target_pairs={{0,15},{1,0},{2,1},{3,2},{4,3},{5,4},{6,5},{7,6},{8,7},{9,8},{10,9... | collective-permute-start | bytes 6488072 | tf_op jit(solution)/gta,gtb->gab/dot_general | solution.py:19
  665.6 48.6 %collective-permute-start.3 = (bf16[1,1,352,3072]{3,2,1,0:T(8,128)(2,1)}, bf16[1,1,352,3072]{3,2,1,0:T(8,128)(2,1)}, u32[]{:S(2)}, u32[]{:S(2)}) collective-permute-start(bf16[1,1,352,3072]{3,2,1,0:T(8,128)(2,1)} %collective-permute-done.2), channel_id=13, source_target_pairs={{0,1},{1,2},{2,3},{3,4},{4,5},{5,6},{6,7},{7,8},{8,9},{9,10},{10,1... | collective-permute-start | bytes 6488072 | tf_op jit(solution)/gta,gtb->gab/dot_general | solution.py:19
  714.2 75.3 %collective-permute-start = (bf16[1,1,352,3072]{3,2,1,0:T(8,128)(2,1)}, bf16[1,1,352,3072]{3,2,1,0:T(8,128)(2,1)S(1)}, u32[]{:S(2)}, u32[]{:S(2)}) collective-permute-start(bf16[1,1,352,3072]{3,2,1,0:T(8,128)(2,1)} %get-tuple-element.84), channel_id=10, source_target_pairs={{0,15},{1,0},{2,1},{3,2},{4,3},{5,4},{6,5},{7,6},{8,7},{9,8},{10,9... | collective-permute-start | bytes 6488072 | tf_op jit(solution)/gta,gtb->gab/dot_general | solution.py:19
  714.2 79.9 %collective-permute-start.2 = (bf16[1,1,352,3072]{3,2,1,0:T(8,128)(2,1)}, bf16[1,1,352,3072]{3,2,1,0:T(8,128)(2,1)}, u32[]{:S(2)}, u32[]{:S(2)}) collective-permute-start(bf16[1,1,352,3072]{3,2,1,0:T(8,128)(2,1)} %get-tuple-element.86), channel_id=11, source_target_pairs={{0,1},{1,2},{2,3},{3,4},{4,5},{5,6},{6,7},{7,8},{8,9},{9,10},{10,1... | collective-permute-start | bytes 6488072 | tf_op jit(solution)/gta,gtb->gab/dot_general | solution.py:19
  789.4 87.2 %collective-permute-start.1 = (bf16[1,1,352,3072]{3,2,1,0:T(8,128)(2,1)S(1)}, bf16[1,1,352,3072]{3,2,1,0:T(8,128)(2,1)}, u32[]{:S(2)}, u32[]{:S(2)}) collective-permute-start(bf16[1,1,352,3072]{3,2,1,0:T(8,128)(2,1)S(1)} %collective-permute-done), channel_id=12, source_target_pairs={{0,15},{1,0},{2,1},{3,2},{4,3},{5,4},{6,5},{7,6},{8,7},{9,8},{10,9... | collective-permute-start | bytes 6488072 | tf_op jit(solution)/gta,gtb->gab/dot_general | solution.py:19
  794.1 85.3 %collective-permute-start.3 = (bf16[1,1,352,3072]{3,2,1,0:T(8,128)(2,1)}, bf16[1,1,352,3072]{3,2,1,0:T(8,128)(2,1)}, u32[]{:S(2)}, u32[]{:S(2)}) collective-permute-start(bf16[1,1,352,3072]{3,2,1,0:T(8,128)(2,1)} %collective-permute-done.2), channel_id=13, source_target_pairs={{0,1},{1,2},{2,3},{3,4},{4,5},{5,6},{6,7},{7,8},{8,9},{9,10},{10,1... | collective-permute-start | bytes 6488072 | tf_op jit(solution)/gta,gtb->gab/dot_general | solution.py:19
  879.4 47.2 %collective-permute-start = (bf16[1,1,352,3072]{3,2,1,0:T(8,128)(2,1)}, bf16[1,1,352,3072]{3,2,1,0:T(8,128)(2,1)S(1)}, u32[]{:S(2)}, u32[]{:S(2)}) collective-permute-start(bf16[1,1,352,3072]{3,2,1,0:T(8,128)(2,1)} %get-tuple-element.84), channel_id=10, source_target_pairs={{0,15},{1,0},{2,1},{3,2},{4,3},{5,4},{6,5},{7,6},{8,7},{9,8},{10,9... | collective-permute-start | bytes 6488072 | tf_op jit(solution)/gta,gtb->gab/dot_general | solution.py:19
  881.3 50.0 %collective-permute-start.2 = (bf16[1,1,352,3072]{3,2,1,0:T(8,128)(2,1)}, bf16[1,1,352,3072]{3,2,1,0:T(8,128)(2,1)}, u32[]{:S(2)}, u32[]{:S(2)}) collective-permute-start(bf16[1,1,352,3072]{3,2,1,0:T(8,128)(2,1)} %get-tuple-element.86), channel_id=11, source_target_pairs={{0,1},{1,2},{2,3},{3,4},{4,5},{5,6},{6,7},{7,8},{8,9},{9,10},{10,1... | collective-permute-start | bytes 6488072 | tf_op jit(solution)/gta,gtb->gab/dot_general | solution.py:19
  926.6 48.7 %collective-permute-start.1 = (bf16[1,1,352,3072]{3,2,1,0:T(8,128)(2,1)S(1)}, bf16[1,1,352,3072]{3,2,1,0:T(8,128)(2,1)}, u32[]{:S(2)}, u32[]{:S(2)}) collective-permute-start(bf16[1,1,352,3072]{3,2,1,0:T(8,128)(2,1)S(1)} %collective-permute-done), channel_id=12, source_target_pairs={{0,15},{1,0},{2,1},{3,2},{4,3},{5,4},{6,5},{7,6},{8,7},{9,8},{10,9... | collective-permute-start | bytes 6488072 | tf_op jit(solution)/gta,gtb->gab/dot_general | solution.py:19
  931.2 45.2 %collective-permute-start.3 = (bf16[1,1,352,3072]{3,2,1,0:T(8,128)(2,1)}, bf16[1,1,352,3072]{3,2,1,0:T(8,128)(2,1)}, u32[]{:S(2)}, u32[]{:S(2)}) collective-permute-start(bf16[1,1,352,3072]{3,2,1,0:T(8,128)(2,1)} %collective-permute-done.2), channel_id=13, source_target_pairs={{0,1},{1,2},{2,3},{3,4},{4,5},{5,6},{6,7},{7,8},{8,9},{9,10},{10,1... | collective-permute-start | bytes 6488072 | tf_op jit(solution)/gta,gtb->gab/dot_general | solution.py:19
  976.4 48.7 %collective-permute-start = (bf16[1,1,352,3072]{3,2,1,0:T(8,128)(2,1)}, bf16[1,1,352,3072]{3,2,1,0:T(8,128)(2,1)S(1)}, u32[]{:S(2)}, u32[]{:S(2)}) collective-permute-start(bf16[1,1,352,3072]{3,2,1,0:T(8,128)(2,1)} %get-tuple-element.84), channel_id=10, source_target_pairs={{0,15},{1,0},{2,1},{3,2},{4,3},{5,4},{6,5},{7,6},{8,7},{9,8},{10,9... | collective-permute-start | bytes 6488072 | tf_op jit(solution)/gta,gtb->gab/dot_general | solution.py:19
  980.0 49.8 %collective-permute-start.2 = (bf16[1,1,352,3072]{3,2,1,0:T(8,128)(2,1)}, bf16[1,1,352,3072]{3,2,1,0:T(8,128)(2,1)}, u32[]{:S(2)}, u32[]{:S(2)}) collective-permute-start(bf16[1,1,352,3072]{3,2,1,0:T(8,128)(2,1)} %get-tuple-element.86), channel_id=11, source_target_pairs={{0,1},{1,2},{2,3},{3,4},{4,5},{5,6},{6,7},{7,8},{8,9},{9,10},{10,1... | collective-permute-start | bytes 6488072 | tf_op jit(solution)/gta,gtb->gab/dot_general | solution.py:19
  1025.1 49.0 %collective-permute-start.1 = (bf16[1,1,352,3072]{3,2,1,0:T(8,128)(2,1)S(1)}, bf16[1,1,352,3072]{3,2,1,0:T(8,128)(2,1)}, u32[]{:S(2)}, u32[]{:S(2)}) collective-permute-start(bf16[1,1,352,3072]{3,2,1,0:T(8,128)(2,1)S(1)} %collective-permute-done), channel_id=12, source_target_pairs={{0,15},{1,0},{2,1},{3,2},{4,3},{5,4},{6,5},{7,6},{8,7},{9,8},{10,9... | collective-permute-start | bytes 6488072 | tf_op jit(solution)/gta,gtb->gab/dot_general | solution.py:19
  1029.7 44.3 %collective-permute-start.3 = (bf16[1,1,352,3072]{3,2,1,0:T(8,128)(2,1)}, bf16[1,1,352,3072]{3,2,1,0:T(8,128)(2,1)}, u32[]{:S(2)}, u32[]{:S(2)}) collective-permute-start(bf16[1,1,352,3072]{3,2,1,0:T(8,128)(2,1)} %collective-permute-done.2), channel_id=13, source_target_pairs={{0,1},{1,2},{2,3},{3,4},{4,5},{5,6},{6,7},{7,8},{8,9},{9,10},{10,1... | collective-permute-start | bytes 6488072 | tf_op jit(solution)/gta,gtb->gab/dot_general | solution.py:19
Sparse Core Ops, SparseCore 0:
  10.4 175.6 all-gather.8
  187.7 172.8 all-gather.10
  416.2 451.4 reduce-scatter.3
where the time goes:
time: 1100 us; the launch traced here: 1090 us
  waiting for transfers between devices  485 us (44%)
  matrix products  477 us (43%)
  other arithmetic  47.7 us (4%)
  local copies, waits for them, and re-layouts  30.6 us (3%)
  starting transfers between devices  29.9 us (3%)
  between operations  14.2 us (1%)
    dot_general x17, waiting for transfers between devices, by_group(): jnp.einsum('gta,gtb->gab', a, b, preferred_element_type=jnp.float32)  309 us
    dot_general x10, matrix products, by_group(): jnp.einsum('gta,gtb->gab', a, b, preferred_element_type=jnp.float32)  283 us
    unnamed x5, waiting for transfers between devices  176 us
    dot_general x2, matrix products, step(): dx = jnp.dot(d_gate, w_gate.T) + jnp.dot(d_up, w_up.T)  130 us
    dot_general x1, matrix products, step(): d_hidden = jnp.dot(dy, w_down.T, preferred_element_type=jnp.float32)  63.6 us
    reshape x1, other arithmetic, by_group(): a, b = (t.reshape(groups, -1, t.shape[-1]) for t in (a, b))  36.4 us
    dot_general x17, starting transfers between devices, by_group(): jnp.einsum('gta,gtb->gab', a, b, preferred_element_type=jnp.float32)  29.8 us
    unnamed x5, local copies, waits for them, and re-layouts  28.3 us
  transfers between devices with their start and end apart: 20, of which 13 were waited for; matrix products, arithmetic and copies ran while one was open for 51% of the time, Pallas kernels for 0%

commit v1 on v0

v1 whole, which is shorter than its diff:
```python
import jax
import jax.numpy as jnp
from jax import lax
from jax.experimental import pallas as pl
from jax.experimental.pallas import tpu as pltpu
from jax.sharding import PartitionSpec as P

R, D, F = 352, 3072, 1536
H = R // 2
RA = 264
RING = 8
NC = 2
CH = F
BF, F32 = jnp.bfloat16, jnp.float32
NT = (((1,), (1,)), ((), ()))
C0, C1 = 0.7978845608028654, 0.044715
TILE = 512
KB = 4 * H


def grads(g, u, dh):
    g, u = g.astype(F32), u.astype(F32)
    g2 = g * g
    t = jnp.tanh(g * (C0 + (C0 * C1) * g2))
    q = 0.5 + 0.5 * t
    gelu = g * q
    slope = q + gelu * ((1.0 - q) * (2.0 * C0 + (6.0 * C0 * C1) * g2))
    return (dh * (u * slope)).astype(BF), (dh * gelu).astype(BF), (gelu * u).astype(BF)


MESH = pl.DeviceIdType.MESH


def place():
    tp = lax.axis_index("tp")
    y, z, c = tp // 8, lax.rem(tp // 2, 4), lax.rem(tp, 2)
    return y, z, c, jnp.where(y == 0, z, 7 - z)


def dev(p, core):
    return (p // 4 * 4 + jnp.where(p < 4, p, 7 - p)) * 2 + core


def start(pos, s, side, core):
    p = lax.rem(pos + RING - s, RING) if side == 0 else lax.rem(pos + s, RING)
    return pl.multiple_of(dev(p, core) * R + side * H, 16)


def mirrored(z):
    return jnp.where(z < 2, z, 3 - z)


def order(zt, other, zs):
    k = jnp.where(zt < 2, zs, 3 - zs)
    o = jnp.where((mirrored(zt) == 1) & (k < 2), 1 - k, k)
    return 2 * o + other


def greet(y, z, c):
    bar = pltpu.get_barrier_semaphore()

    def hello(d):
        pl.semaphore_signal(bar, inc=1, device_id={"tp": d}, device_id_type=MESH)
    hello((y * 4 + z) * 2 + 1 - c)
    hello(((1 - y) * 4 + z) * 2 + c)

    @pl.when(z < 3)
    def _():
        hello((y * 4 + z + 1) * 2 + c)

    @pl.when(z > 0)
    def _():
        hello((y * 4 + z - 1) * 2 + c)
    pl.semaphore_wait(bar, 2 + jnp.where(z < 3, 1, 0) + jnp.where(z > 0, 1, 0))


def remote(src, dst, ss, rs, d):
    return pltpu.make_async_remote_copy(src, dst, ss, rs, device_id={"tp": d}, device_id_type=MESH)


def arrived(sem, dst):
    pltpu.make_async_copy(dst, dst, sem).wait()


XPARTS = ((0, RA), (RA, R - RA))
PIECE = 88
BOTH = (0, 1)


def xplace(zt, other, zs, part, mine):
    r0, n = XPARTS[part]
    return pl.ds(pl.multiple_of(order(zt, other, zs) * KB + (0 if mine else R) + r0, 8), n)


def back_kernel(x, dy, gate, up, wd, wg, wu,
                h, dyf, dgo, pf, qb, xf,
                wdv, wgu, dyb, gb, ub, dgu, hb, pv, qs,
                w_s, ld_s, own_s, o_s, p_s, ag_r, ag_t, dd_r, dd_t, q_r, q_t, x_r, x_t):
    y, z, c, pos = place()
    right, left, mate = dev(lax.rem(pos + 1, RING), c), dev(lax.rem(pos + RING - 1, RING), c), dev(pos, 1 - c)
    dirs = (right, left)

    def rows(s, side, core):
        return pl.ds(start(pos, s, side, core), H)

    def slab(s, side, part, mine):
        return dyf.at[pl.ds(pl.multiple_of(s * KB + (0 if mine else R) + side * H + part * PIECE, 8), PIECE)]

    def block(s, mine):
        return pl.ds(pl.multiple_of(s * KB + (0 if mine else R), 16), R)

    def ring_copy(src, s, side, part):
        return remote(src, slab(s, side, part, True), ag_t.at[s, side, part], ag_r.at[s, side, part], dirs[side])

    def mate_copy(src, s, side, part):
        return remote(src, slab(s, side, part, False), dd_t.at[s, side, part], dd_r.at[s, side, part], mate)

    weights = [pltpu.make_async_copy(wd, wdv, w_s.at[0]),
               pltpu.make_async_copy(wg, wgu.at[:, pl.ds(0, F)], w_s.at[1]),
               pltpu.make_async_copy(wu, wgu.at[:, pl.ds(F, F)], w_s.at[2])]

    def loads(s, slot, first=False):
        core = c if slot == 1 else 1 - c
        out = [pltpu.make_async_copy(dy if first else dyf.at[block(s, slot == 1)], dyb.at[slot], ld_s.at[slot, 4])]
        for side in BOTH:
            half, r = pl.ds(side * H, H), rows(s, side, core)
            out += [pltpu.make_async_copy(gate.at[r], gb.at[slot, half], ld_s.at[slot, 2 * side]),
                    pltpu.make_async_copy(up.at[r], ub.at[slot, half], ld_s.at[slot, 2 * side + 1])]
        return out

    def stores(s, slot):
        out = [pltpu.make_async_copy(hb, h.at[block(s, slot == 1)], o_s.at[2])]
        for side in BOTH:
            p = lax.rem(pos + RING - s, RING) if side == 0 else lax.rem(pos + s, RING)
            zs = jnp.where(p < 4, p, 7 - p)
            other = jnp.where(p // 4 == y, 0, 1)
            to = order(z, other, zs) * KB + (0 if slot == 1 else R) + side * H
            out.append(pltpu.make_async_copy(dgu.at[pl.ds(side * H, H)], dgo.at[pl.ds(pl.multiple_of(to, 16), H)],
                                             o_s.at[side]))
        return out

    def dhidden(slot):
        a = dyb[slot]
        for n in range(F // TILE):
            cs = pl.ds(n * TILE, TILE)
            dh = lax.dot_general(a, wdv[n * TILE:(n + 1) * TILE, :], NT, preferred_element_type=F32)
            dg, du, hid = grads(gb[slot, :, cs], ub[slot, :, cs], dh)
            dgu[:, cs] = dg
            dgu[:, pl.ds(F + n * TILE, TILE)] = du
            hb[:, cs] = hid

    def partial_dx(j, store):
        a = dgu[...]
        for n in range(CH // TILE):
            r0 = j * CH + n * TILE
            store(r0, lax.dot_general(a, wgu[r0:r0 + TILE, :], NT, preferred_element_type=F32))

    def q_send(s, j):
        return remote(qs.at[j], qb.at[s, :, pl.ds(j * CH, CH)], q_t.at[j], q_r.at[s, j], mate)

    def p_store(s, j):
        cols = pl.ds(j * CH, CH)
        return pltpu.make_async_copy(pv.at[:, cols], pf.at[s, :, cols], p_s.at[j])

    ways = ((z < 3, (y * 4 + z + 1) * 2 + c, 0, z + 1), (z > 0, (y * 4 + z - 1) * 2 + c, 0, z - 1),
            (z >= 0, ((1 - y) * 4 + z) * 2 + c, 1, z))

    def x_send(w, part):
        r0, n = XPARTS[part]
        _, target, other, zt = ways[w]
        return remote(x.at[pl.ds(r0, n)], xf.at[xplace(zt, other, z, part, True)], x_t.at[w, part], x_r.at[w, part], target)

    def x_mate(part):
        r0, n = XPARTS[part]
        return remote(x.at[pl.ds(r0, n)], xf.at[xplace(z, 0, z, part, False)], x_t.at[3, part], x_r.at[3, part], mate)

    weights[0].start()
    for cp in loads(0, 1, True):
        cp.start()
    own_x = [pltpu.make_async_copy(x, dyb.at[0], own_s.at[0]),
             pltpu.make_async_copy(dyb.at[0], xf.at[pl.ds(pl.multiple_of(order(z, 0, z) * KB, 16), R)], own_s.at[0])]
    own_x[0].start()
    own_dy = pltpu.make_async_copy(dyb.at[1], dyf.at[pl.ds(0, R)], own_s.at[1])
    greet(y, z, c)

    for part in BOTH:
        for side in BOTH:
            src = dy.at[pl.ds(side * H + part * PIECE, PIECE)]
            ring_copy(src, 1, side, part).start()
            mate_copy(src, 0, side, part).start()

    weights[0].wait()
    weights[1].start()
    weights[2].start()
    own_x[0].wait()
    own_x[1].start()

    def advance(s, part):
        @pl.when(s < RING - 1)
        def _():
            for side in BOTH:
                p = slab(s + 1, side, part, True)
                arrived(ag_r.at[s + 1, side, part], p)

                @pl.when(s < RING - 2)
                def _():
                    ring_copy(p, s + 2, side, part).start()
                mate_copy(p, s + 1, side, part).start()

    def x_leaves(part):
        for w in range(3):
            @pl.when(ways[w][0])
            def _():
                x_send(w, part).start()
        x_mate(part).start()

    def step(s, carry):
        for cp in loads(s, 1):
            cp.wait()

        @pl.when(s == 0)
        def _():
            own_dy.start()

        @pl.when(s > 0)
        def _():
            for cp in stores(s, 0):
                cp.wait()
            for j in range(NC):
                p_store(s, j).wait()
        dhidden(1)
        for cp in stores(s, 1):
            cp.start()

        @pl.when(s == 0)
        def _():
            own_dy.wait()
            own_x[1].wait()
            weights[1].wait()
            weights[2].wait()

        @pl.when(s < RING - 1)
        def _():
            for cp in loads(s + 1, 1)[1:]:
                cp.start()
        for part in BOTH:
            for side in BOTH:
                arrived(dd_r.at[s, side, part], slab(s, side, part, False))
        for cp in loads(s, 0):
            cp.start()

        def put_p(c0, v):
            pv[:, pl.ds(c0, TILE)] = v
        for j in range(NC):
            partial_dx(j, put_p)
            p_store(s, j).start()
        advance(s, 0)

        for cp in loads(s, 0):
            cp.wait()
        for cp in stores(s, 1):
            cp.wait()

        @pl.when(s > 0)
        def _():
            for j in range(NC):
                q_send(s, j).wait_send()

        def put_q(c0, v):
            qs[c0 // CH, :, pl.ds(c0 % CH, TILE)] = v.astype(BF)
        dhidden(0)
        partial_dx(0, put_q)
        for cp in stores(s, 0):
            cp.start()
        q_send(s, 0).start()
        advance(s, 1)

        @pl.when(s < RING - 1)
        def _():
            loads(s + 1, 1)[0].start()
        for part in BOTH:
            @pl.when(s == XSTEPS[part])
            def _():
                x_leaves(part)
        partial_dx(1, put_q)
        q_send(s, 1).start()
        return carry

    lax.fori_loop(0, RING, step, 0)

    for cp in stores(RING - 1, 0):
        cp.wait()
    for j in range(NC):
        p_store(0, j).wait()
        q_send(0, j).wait_send()
    comes = (z > 0, z < 3, z >= 0)
    for part in BOTH:
        n = XPARTS[part][1]
        for w in range(3):
            @pl.when(comes[w])
            def _():
                arrived(x_r.at[w, part], xf.at[pl.ds(0, n)])

            @pl.when(ways[w][0])
            def _():
                x_send(w, part).wait_send()
        arrived(x_r.at[3, part], xf.at[pl.ds(0, n)])
        x_mate(part).wait_send()

    def drain(s, carry):
        for part in BOTH:
            for side in BOTH:
                p = slab(0, side, part, True)

                @pl.when(s > 0)
                def _():
                    ring_copy(p, s, side, part).wait_send()
                mate_copy(p, s, side, part).wait_send()
        for j in range(NC):
            arrived(q_r.at[s, j], qb.at[0, :, pl.ds(j * CH, CH)])
        return carry
    lax.fori_loop(0, RING, drain, 0)


XSTEPS = (5, 5)


def back_call(x, dy, gate, up, wd, wg, wu):
    sd = jax.ShapeDtypeStruct
    hbm = pl.BlockSpec(memory_space=pl.ANY)
    outs = [sd((16 * R, F), BF), sd((16 * R, D), BF), sd((16 * R, 2 * F), BF), sd((RING, R, D), F32),
            sd((RING, R, D), BF), sd((16 * R, D), BF)]
    dma = pltpu.SemaphoreType.DMA
    return pl.pallas_call(
        back_kernel,
        out_shape=outs,
        in_specs=[hbm] * 7,
        out_specs=[hbm] * len(outs),
        scratch_shapes=[
            pltpu.VMEM((F, D), BF), pltpu.VMEM((D, 2 * F), BF),
            pltpu.VMEM((2, R, D), BF), pltpu.VMEM((2, R, F), BF), pltpu.VMEM((2, R, F), BF),
            pltpu.VMEM((R, 2 * F), BF), pltpu.VMEM((R, F), BF),
            pltpu.VMEM((R, D), F32), pltpu.VMEM((NC, R, CH), BF),
            dma((3,)), dma((2, 5)), dma((2,)), dma((3,)), dma((NC,)),
            dma((RING, 2, 2)), dma((RING, 2, 2)), dma((RING, 2, 2)), dma((RING, 2, 2)),
            dma((RING, NC)), dma((NC,)), dma((4, 2)), dma((4, 2)),
        ],
        compiler_params=pltpu.CompilerParams(collective_id=0, has_side_effects=True, vmem_limit_bytes=66_000_000),
        cost_estimate=pl.CostEstimate(flops=3 * 2 * 16 * R * D * F, bytes_accessed=300_000_000, transcendentals=16 * R * F),
        name="back",
    )(x, dy, gate, up, wd, wg, wu)


TN = (((0,), (0,)), ((), ()))
BLK = 512
NB = 16 * R // BLK
WIDE = 256
CAST = 128
SLOTS = 6
TALL = 768
TALLS = F // TALL
DOWN = NB * TALLS
DOWN_OUT = DOWN + 2
GU = 2 * DOWN
GU_OUT = 4
ENDS = (
    "CJIDSZYTZYZZZyZYUZYZZzZYVZYZZEKmZYZZZLoZYZZFZpZYZZ"
    "QZYuZYZZnZYRZYZZGMvZYZZZNkZYZZZHlZYZZZPiZYwZYZZjZY"
    "xZYZOeZYsZYZZgZYtZYZZhZYqZYZZfZYcZYrZYZZZdZYaZYZbY"
)
INNER = (
    "AELBFKZZZZZJZZZZZZZZZGIZZZZNSZYZZZHTZYZZPMZyZYZZZz"
    "ZYZUZYmZYZZVZOYZZZQZYoZYnZYqZYRZYpZYrZYsZYkZZZYtZY"
    "lZYaZZYwZYiZYcZYxZYjZZZYuZYdZYZZvZYbZYgZYZeZYhZYfY"
)
LETTERS = "ZABCDEFGHIJKLMNOPabcdefghijklmnopqrstuvwxyzQRSTUVY"
SUMS = LETTERS.index("a")
ADD = LETTERS.index("Y")
BASE = 64
PER = 5
ITEMS = len(ENDS)


def packed(work):
    codes = [LETTERS.index(w) for w in work] + [0] * (-len(work) % PER)
    return [sum(code * BASE**j for j, code in enumerate(codes[i:i + PER])) for i in range(0, len(codes), PER)]


def chosen(table, i):
    v = table[0]
    for n, entry in enumerate(table[1:], 1):
        v = jnp.where(i == n, entry, v)
    return v


def reduce_kernel(xin, h, dyf, dgu, pf, qb,
                  xf, lo, hi, iy, dx, og, ou, od,
                  acc, xs, ds, st, pb, ib, ob,
                  x_r, x_t, xd_r, xd_t, lo_r, hi_r, iy_r, ob_s, ld_s, st_s, in_s):
    y, z, c, pos = place()
    end = mirrored(z) == 0
    above, below, across, mate = ((y * 4 + z + 1) * 2 + c, (y * 4 + z - 1) * 2 + c,
                                  ((1 - y) * 4 + z) * 2 + c, (y * 4 + z) * 2 + 1 - c)

    def real(k):
        return jnp.where(z < 2, k, 3 - k)

    def x_sends(other, zs, part):
        src = xf.at[xplace(z, other, zs, part, True)]
        n = other * 4 + zs
        turn = (other == 1) & (zs == z)
        if part == 0:
            go_up, go_down, go_over = (other == 0) & (zs < z), (other == 0) & (zs > z), other == 0
        else:
            go_up, go_down, go_over = (zs < z) | turn, (zs > z) | turn, None
        out = [(go_up & (z < 3), remote(src, xf.at[xplace(z + 1, other, zs, part, True)], x_t.at[0, n, part],
                                        x_r.at[n, part], above)),
               (go_down & (z > 0), remote(src, xf.at[xplace(z - 1, other, zs, part, True)], x_t.at[1, n, part],
                                          x_r.at[n, part], below)),
               (z >= 0, remote(src, xf.at[xplace(z, other, zs, part, False)], xd_t.at[n, part], xd_r.at[n, part], mate))]
        if go_over is not None:
            out.append((go_over, remote(src, xf.at[xplace(z, 1 - other, zs, part, True)], x_t.at[2, n, part],
                                        x_r.at[(1 - other) * 4 + zs, part], across)))
        return out

    def pass_on(other, zs, part):
        first = ((other == 0) & ((zs - z) * (zs - z) == 1)) | ((other == 1) & (zs == z))

        @pl.when(jnp.logical_not(first))
        def _():
            arrived(x_r.at[other * 4 + zs, part], xf.at[xplace(z, other, zs, part, True)])
        for cond, cp in x_sends(other, zs, part):
            @pl.when(cond)
            def _():
                cp.start()

    def slot_from_mate(sl, carry):
        o, other = sl // 2, lax.rem(sl, 2)
        k = jnp.where(end | (o > 1), o, 1 - o)
        for part in BOTH:
            arrived(xd_r.at[other * 4 + real(k), part], xf.at[pl.ds(0, XPARTS[part][1])])
        return carry

    def down_loads(b, slot):
        r = pl.ds(pl.multiple_of(b * BLK, 16), BLK)
        return [pltpu.make_async_copy(h.at[r], xs.at[slot, :, pl.ds(0, F)], ld_s.at[slot, 0]),
                pltpu.make_async_copy(dyf.at[r], ds.at[slot], ld_s.at[slot, 1])]

    def loads(b, slot):
        r = pl.ds(pl.multiple_of(b * BLK, 16), BLK)
        return [pltpu.make_async_copy(xf.at[r], xs.at[slot], ld_s.at[slot, 2]),
                pltpu.make_async_copy(dgu.at[r], ds.at[slot], ld_s.at[slot, 3])]

    def product(slot, m, first):
        rows = pl.ds(pl.multiple_of(m * TALL, TALL), TALL)
        a = xs[slot, :, rows]
        for n in range(2 * F // WIDE):
            cols = pl.ds(n * WIDE, WIDE)
            r = lax.dot_general(a, ds[slot, :, cols], TN, preferred_element_type=F32)
            acc[rows, cols] = jnp.where(first, 0.0, acc[rows, cols]) + r

    def last_slot(b):
        return (BLK * (b + 1) - 1) // KB

    def down_copy(i, slot):
        return [pltpu.make_async_copy(st.at[slot], od.at[pl.ds(pl.multiple_of(i * CAST, 16), CAST)], st_s.at[slot, 0])]

    def weight_copies(i, slot):
        r = pl.ds(pl.multiple_of(i * CAST, 16), CAST)
        return [pltpu.make_async_copy(st.at[slot, :, pl.ds(0, F)], og.at[r], st_s.at[slot, 0]),
                pltpu.make_async_copy(st.at[slot, :, pl.ds(F, F)], ou.at[r], st_s.at[slot, 1])]

    def cast(n, part, parts, copies):
        def one(i, carry):
            slot = lax.rem(i, 2)

            @pl.when(i > 1)
            def _():
                for cp in copies(i, slot):
                    cp.wait()
            st[slot] = acc[pl.ds(pl.multiple_of(i * CAST, 16), CAST), :].astype(BF)
            for cp in copies(i, slot):
                cp.start()
            return carry
        lax.fori_loop(part * (n // parts), (part + 1) * (n // parts), one, 0)

        @pl.when(part == parts - 1)
        def _():
            for i in (n - 2, n - 1):
                for cp in copies(i, i % 2):
                    cp.wait()

    def unit(u):
        v = u - DOWN_OUT
        gu = (v >= 0) & (v < GU)
        b = jnp.where(gu, v // (2 * TALLS), u // TALLS)
        m = jnp.where(gu, lax.rem(v, 2 * TALLS), lax.rem(u, TALLS))
        slot = lax.rem(b + jnp.where(gu, NB, 0), 2)

        @pl.when((u < DOWN) & (m == 0))
        def _():
            for cp in down_loads(b, slot):
                cp.wait()

            @pl.when(b < NB - 1)
            def _():
                for cp in down_loads(b + 1, 1 - slot):
                    cp.start()

            @pl.when(b == NB - 1)
            def _():
                for cp in loads(0, 1 - slot):
                    cp.start()

        @pl.when(gu & (m == 0))
        def _():
            for cp in loads(b, slot):
                cp.wait()

        @pl.when(gu & (m == TALLS) & (b < NB - 1))
        def _():
            lax.fori_loop(last_slot(b) + 1, last_slot(b + 1) + 1, slot_from_mate, 0)
            for cp in loads(b + 1, 1 - slot):
                cp.start()

        @pl.when((u < DOWN) | gu)
        def _():
            product(slot, m, b == 0)

        @pl.when((u >= DOWN) & (v < 0))
        def _():
            cast(F // CAST, u - DOWN, DOWN_OUT - DOWN, down_copy)

        @pl.when(v >= GU)
        def _():
            cast(D // CAST, v - GU, GU_OUT, weight_copies)

    def target(other, zd, piece):
        yd = jnp.where(other == 0, y, 1 - y)
        along = (piece < 2) | (other == 0)
        from_below = along & (z > 0) & (zd >= z)
        from_above = along & (z < 3) & (zd <= z)
        from_over = (other == 0) & ((piece > 1) | (zd == z))
        return yd * 4 + zd, pl.ds(pl.multiple_of(piece * PIECE, 8), PIECE), along, from_below, from_above, from_over

    def sum_loads(other, zd, piece):
        dc, rows, _, from_below, from_above, from_over = target(other, zd, piece)
        pd = jnp.where(dc < 4, zd, 7 - zd)
        s = lax.rem(jnp.where(piece < 2, pos - pd, pd - pos) + RING, RING)
        return [(z >= 0, pltpu.make_async_copy(pf.at[s, rows], pb, in_s.at[0])),
                (z >= 0, pltpu.make_async_copy(qb.at[s, rows], ib.at[0], in_s.at[1])),
                (from_below, pltpu.make_async_copy(lo.at[dc, rows], ib.at[1], in_s.at[2])),
                (from_above, pltpu.make_async_copy(hi.at[dc, rows], ib.at[2], in_s.at[3])),
                (from_over, pltpu.make_async_copy(iy.at[dc, rows], ib.at[3], in_s.at[4]))]

    def sum_load(other, zd, piece):
        dc, rows, _, from_below, from_above, from_over = target(other, zd, piece)
        for cond, sem, buf in ((from_below, lo_r, lo), (from_above, hi_r, hi), (from_over, iy_r, iy)):
            @pl.when(cond)
            def _():
                arrived(sem.at[dc, piece], buf.at[dc, rows])
        for cond, cp in sum_loads(other, zd, piece):
            @pl.when(cond)
            def _():
                cp.start()

    def out_wait(slot):
        pltpu.make_async_copy(ob.at[slot], ob.at[slot], ob_s.at[slot]).wait()

    def sum_send(other, zd, piece, n):
        dc, rows, along, from_below, from_above, from_over = target(other, zd, piece)
        slot = lax.rem(n, SLOTS)
        for cond, cp in sum_loads(other, zd, piece):
            @pl.when(cond)
            def _():
                cp.wait()

        @pl.when(n >= SLOTS)
        def _():
            out_wait(slot)
        for i, cond in ((1, from_below), (2, from_above), (3, from_over)):
            @pl.when(cond)
            def _():
                pb[...] = pb[...] + ib[i].astype(F32)
        ob[slot] = (pb[...] + ib[0].astype(F32)).astype(BF)
        here = along & (zd == z)
        sem = ob_s.at[slot]

        @pl.when(along & (zd > z))
        def _():
            remote(ob.at[slot], lo.at[dc, rows], sem, lo_r.at[dc, piece], above).start()

        @pl.when(along & (zd < z))
        def _():
            remote(ob.at[slot], hi.at[dc, rows], sem, hi_r.at[dc, piece], below).start()

        @pl.when(jnp.logical_not(along) | (here & (other == 1)))
        def _():
            remote(ob.at[slot], iy.at[dc, rows], sem, iy_r.at[dc, piece], across).start()

        @pl.when(here & (other == 0))
        def _():
            pltpu.make_async_copy(ob.at[slot], dx.at[rows], sem).start()

    for cp in down_loads(0, 0):
        cp.start()
    greet(y, z, c)
    tables = packed(ENDS), packed(INNER)

    def item(i, carry):
        u, n, held = carry
        word = jnp.where(end, *(chosen(t, i // PER) for t in tables))
        code = lax.rem(word, BASE)
        for j in range(1, PER):
            code = jnp.where(lax.rem(i, PER) == j, lax.rem(word // BASE**j, BASE), code)

        def piece_of(index):
            return index // 16, real(lax.rem(index // 4, 4)), lax.rem(index, 4)

        @pl.when(code == 0)
        def _():
            unit(u)
        for part in BOTH:
            @pl.when((code > 0) & (code < SUMS) & (lax.rem(code + 1, 2) == part))
            def _():
                pass_on((code - 1) // 8, real(lax.rem((code - 1) // 2, 4)), part)

        @pl.when((code >= SUMS) & (code < ADD))
        def _():
            sum_load(*piece_of(code - SUMS))

        @pl.when(code == ADD)
        def _():
            sum_send(*piece_of(held), n)
        loaded = (code >= SUMS) & (code < ADD)
        return u + jnp.where(code == 0, 1, 0), n + jnp.where(code == ADD, 1, 0), jnp.where(loaded, code - SUMS, held)

    lax.fori_loop(0, ITEMS, item, (jnp.int32(0),) * 3)

    for slot in range(SLOTS):
        out_wait(slot)

    def drain(n, carry):
        other, zs = n // 4, lax.rem(n, 4)

        @pl.when((other == 1) | (zs != z))
        def _():
            for part in BOTH:
                for cond, cp in x_sends(other, zs, part):
                    @pl.when(cond)
                    def _():
                        cp.wait_send()
        return carry
    lax.fori_loop(0, RING, drain, 0)


def reduce_call(xf, h, dyf, dgu, pf, qb):
    sd = jax.ShapeDtypeStruct
    hbm = pl.BlockSpec(memory_space=pl.ANY)
    land = sd((RING, R, D), BF)
    outs = [sd((16 * R, D), BF), land, land, land, sd((R, D), BF), sd((D, F), BF), sd((D, F), BF), sd((F, D), BF)]
    dma = pltpu.SemaphoreType.DMA
    return pl.pallas_call(
        reduce_kernel,
        out_shape=outs,
        in_specs=[hbm] * 6,
        out_specs=[hbm] * len(outs),
        input_output_aliases={0: 0},
        scratch_shapes=[
            pltpu.VMEM((D, 2 * F), F32), pltpu.VMEM((2, BLK, D), BF), pltpu.VMEM((2, BLK, 2 * F), BF),
            pltpu.VMEM((2, CAST, D), BF), pltpu.VMEM((PIECE, D), F32), pltpu.VMEM((4, PIECE, D), BF),
            pltpu.VMEM((SLOTS, PIECE, D), BF),
            dma((RING, 2)), dma((3, RING, 2)), dma((RING, 2)), dma((RING, 2)),
            dma((RING, 4)), dma((RING, 4)), dma((RING, 4)), dma((SLOTS,)), dma((2, 4)), dma((2, 2)), dma((5,)),
        ],
        compiler_params=pltpu.CompilerParams(collective_id=1, has_side_effects=True, vmem_limit_bytes=66_000_000),
        cost_estimate=pl.CostEstimate(flops=3 * 2 * 16 * R * D * F, bytes_accessed=300_000_000, transcendentals=0),
        name="reduce",
    )(xf, h, dyf, dgu, pf, qb)


def copy_kernel(*refs):
    n = len(refs) // 2
    for a, b in zip(refs[:n], refs[n:]):
        b[...] = a[...]


def copy_call(dx, og, ou, od):
    n = 6
    specs = [pl.BlockSpec((R, D // n), lambda i: (0, i)), pl.BlockSpec((D // n, F), lambda i: (i, 0)),
             pl.BlockSpec((D // n, F), lambda i: (i, 0)), pl.BlockSpec((F // n, D), lambda i: (i, 0))]
    return pl.pallas_call(
        copy_kernel,
        grid=(n,),
        out_shape=[jax.ShapeDtypeStruct(a.shape, a.dtype) for a in (dx, og, ou, od)],
        in_specs=specs,
        out_specs=specs,
        compiler_params=pltpu.CompilerParams(dimension_semantics=("arbitrary",), vmem_limit_bytes=66_000_000),
        cost_estimate=pl.CostEstimate(flops=1_000_000, bytes_accessed=61_000_000, transcendentals=0),
        name="copy",
    )(dx, og, ou, od)


def solution(mesh):
    def body(x, dy, gate, up, w_gate, w_up, w_down):
        h, dyf, dgu, pf, qb, xf = back_call(x, dy, gate, up, w_down, w_gate, w_up)
        outs = reduce_call(xf, h, dyf, dgu, pf, qb)
        return tuple(copy_call(*outs[4:]))

    rows, cols = P(("dp", "tp")), P("dp", "tp")
    return jax.shard_map(
        body, mesh=mesh,
        in_specs=(rows, rows, cols, cols, P(None, "tp"), P(None, "tp"), P("tp")),
        out_specs=(rows, cols, cols, P(("dp", "tp"))),
        check_vma=False,
    )
```

time: 1100 us -> 464 us (0.42)
  waiting for transfers between devices: 485 us -> 0 us
  matrix products: 477 us -> 0 us
  Pallas kernels: 0 us -> 463 us
  other arithmetic: 47.7 us -> 0 us
  local copies, waits for them, and re-layouts: 30.6 us -> 0 us
  starting transfers between devices: 29.9 us -> 0 us
  between operations: 14.2 us -> 0.65 us
    dot_general x13 -> x0, matrix products: 477 us -> none  [the longest x10 283 us: by_group(): jnp.einsum('gta,gtb->gab', a, b, preferred_element_type=jnp.float32)]
    pallas_call x0 -> x3, Pallas kernels: none -> 463 us  [the longest x1 228 us: reduce_call(): pl.pallas_call(reduce_kernel, out_shape=outs, in_specs=[hbm] * 6, out_spe...]
    dot_general x17 -> x0, waiting for transfers between devices: 309 us -> none  [by_group(): jnp.einsum('gta,gtb->gab', a, b, preferred_element_type=jnp.float32)]
    unnamed x5 -> x0, waiting for transfers between devices: 176 us -> none
    reshape x2 -> x0, other arithmetic: 47.7 us -> none  [the longest x1 36.4 us: by_group(): a, b = (t.reshape(groups, -1, t.shape[-1]) for t in (a, b))]
    dot_general x17 -> x0, starting transfers between devices: 29.8 us -> none  [by_group(): jnp.einsum('gta,gtb->gab', a, b, preferred_element_type=jnp.float32)]
    unnamed x5 -> x0, local copies, waits for them, and re-layouts: 28.3 us -> none
  transfers between devices with their start and end apart: 20 -> 0, of which waited for: 13 -> 0; matrix products, arithmetic and copies ran while one was open for 51% -> 0% of each run, Pallas kernels for 0% -> 0%
where the time goes in v1:
time: 464 us
  Pallas kernels  463 us (100%)
    pallas_call x1, Pallas kernels, reduce_call(): pl.pallas_call(reduce_kernel, out_shape=outs, in_specs=[hbm] * 6, out_spe...  228 us
    pallas_call x1, Pallas kernels, back_call(): pl.pallas_call(back_kernel, out_shape=outs, in_specs=[hbm] * 7, out_specs...  216 us
    pallas_call x1, Pallas kernels, copy_call(): pl.pallas_call(copy_kernel, grid=(n,), out_shape=[jax.ShapeDtypeStruct(a....  19.8 us

profile of v1, /device:TPU:0, one launch (start us, length us, event | category | flops | bytes accessed | tf_op | source)
XLA Modules:
  0.0 463.9 jit_solution(11319277452891878090)
XLA Ops:
  0.6 215.5 %back.1 = (bf16[5632,1536]{1,0:T(8,128)(2,1)}, bf16[5632,3072]{1,0:T(8,128)(2,1)}, bf16[5632,3072]{1,0:T(8,128)(2,1)}, f32[8,352,3072]{2,1,0:T(8,128)}, bf16[8,3...) custom-call(bf16[352,3072]{1,0:T(8,128)(2,1)} %x.1, bf16[352,3072]{1,0:T(8,128)(2,1)} %dy.1, bf16[5632,1536]{1,0:T(8,128)(2,1)} %gate.1, ...), custom_call_target="tpu_custom_call" | custom-call | flops 159450660864 | bytes 300000000 | tf_op jit(solution)/shard_map/back/pallas_call | solution.py:334
  216.1 228.0 %reduce.1 = (bf16[5632,3072]{1,0:T(8,128)(2,1)}, bf16[8,352,3072]{2,1,0:T(8,128)(2,1)}, bf16[8,352,3072]{2,1,0:T(8,128)(2,1)}, bf16[8,352,3072]{2,1,0:T(8,128)(2...) custom-call(bf16[5632,3072]{1,0:T(8,128)(2,1)} %get-tuple-element.14, ...), custom_call_target="tpu_custom_call", output_to_operand_aliasing={{0}: (0, {})} | custom-call | flops 159450660864 | bytes 300000000 | tf_op jit(solution)/shard_map/reduce/pallas_call | solution.py:663
  444.1 19.8 %copy.14 = (bf16[352,3072]{1,0:T(8,128)(2,1)}, bf16[3072,1536]{1,0:T(8,128)(2,1)}, bf16[3072,1536]{1,0:T(8,128)(2,1)}, bf16[1536,3072]{1,0:T(8,128)(2,1)}) custom-call(bf16[352,3072]{1,0:T(8,128)(2,1)} %get-tuple-element.20.refs_0_, bf16[3072,1536]{1,0:T(8,128)(2,1)} %get-tuple-element.21.refs_1_, bf16[3072,1536]{1,0:T(8,128)(2,1)} %get-tuple-element.22.refs_2_, ...), custom_call_target="tpu_custom_call" | custom-call | flops 1000000 | bytes 61000000 | tf_op jit(solution)/shard_map/copy/pallas_call | solution.py:692

commit v2 on v1

--- a/solution.py
+++ b/solution.py
@@ -363,16 +363,16 @@
 DOWN_OUT = DOWN + 2
 GU = 2 * DOWN
 GU_OUT = 4
-ENDS = (
-    "CJIDSZYTZYZZZyZYUZYZZzZYVZYZZEKmZYZZZLoZYZZFZpZYZZ"
-    "QZYuZYZZnZYRZYZZGMvZYZZZNkZYZZZHlZYZZZPiZYwZYZZjZY"
-    "xZYZOeZYsZYZZgZYtZYZZhZYqZYZZfZYcZYrZYZZZdZYaZYZbY"
-)
-INNER = (
-    "AELBFKZZZZZJZZZZZZZZZGIZZZZNSZYZZZHTZYZZPMZyZYZZZz"
-    "ZYZUZYmZYZZVZOYZZZQZYoZYnZYqZYRZYpZYrZYsZYkZZZYtZY"
-    "lZYaZZYwZYiZYcZYxZYjZZZYuZYdZYZZvZYbZYgZYZeZYhZYfY"
-)
+ENDS = "".join((
+    "CJIDSZYTZYZZZyZYUZYZZzZYVZYZZEKmZYZZZLoZYZZFZpZYZZ",
+    "QZYuZYZZnZYRZYZZGMvZYZZZNkZYZZZHlZYZZZPiZYwZYZZjZY",
+    "xZYZOeZYsZYZZgZYtZYZZhZYqZYZZfZYcZYrZYZZZdZYaZYZbY",
+))
+INNER = "".join((
+    "AELBFKZZZZZJZZZZZZZZZGIZZZZNSZYZZZHTZYZZPMZyZYZZZz",
+    "ZYZUZYmZYZZVZOYZZZQZYoZYnZYqZYRZYpZYrZYsZYkZZZYtZY",
+    "lZYaZZYwZYiZYcZYxZYjZZZYuZYdZYZZvZYbZYgZYZeZYhZYfY",
+))
 LETTERS = "ZABCDEFGHIJKLMNOPabcdefghijklmnopqrstuvwxyzQRSTUVY"
 SUMS = LETTERS.index("a")
 ADD = LETTERS.index("Y")
@@ -685,8 +685,11 @@
         b[...] = a[...]
 
 
+COPIES = 6
+
+
 def copy_call(dx, og, ou, od):
-    n = 6
+    n = COPIES
     specs = [pl.BlockSpec((R, D // n), lambda i: (0, i)), pl.BlockSpec((D // n, F), lambda i: (i, 0)),
              pl.BlockSpec((D // n, F), lambda i: (i, 0)), pl.BlockSpec((F // n, D), lambda i: (i, 0))]
     return pl.pallas_call(

time: 464 us -> 464 us (level)
  no operation moved by 1% of the time
where the time goes in v2:
time: 464 us
  Pallas kernels  463 us (100%)
    pallas_call x1, Pallas kernels, reduce_call(): pl.pallas_call(reduce_kernel, out_shape=outs, in_specs=[hbm] * 6, out_spe...  228 us
    pallas_call x1, Pallas kernels, back_call(): pl.pallas_call(back_kernel, out_shape=outs, in_specs=[hbm] * 7, out_specs...  216 us
    pallas_call x1, Pallas kernels, copy_call(): pl.pallas_call(copy_kernel, grid=(n,), out_shape=[jax.ShapeDtypeStruct(a....  19.8 us

profile of v2, /device:TPU:0, one launch (start us, length us, event | category | flops | bytes accessed | tf_op | source)
XLA Modules:
  0.0 463.9 jit_solution(11319277452891878090)
XLA Ops:
  0.6 215.5 %back.1 = (bf16[5632,1536]{1,0:T(8,128)(2,1)}, bf16[5632,3072]{1,0:T(8,128)(2,1)}, bf16[5632,3072]{1,0:T(8,128)(2,1)}, f32[8,352,3072]{2,1,0:T(8,128)}, bf16[8,3...) custom-call(bf16[352,3072]{1,0:T(8,128)(2,1)} %x.1, bf16[352,3072]{1,0:T(8,128)(2,1)} %dy.1, bf16[5632,1536]{1,0:T(8,128)(2,1)} %gate.1, ...), custom_call_target="tpu_custom_call" | custom-call | flops 159450660864 | bytes 300000000 | tf_op jit(solution)/shard_map/back/pallas_call | solution.py:334
  216.1 228.0 %reduce.1 = (bf16[5632,3072]{1,0:T(8,128)(2,1)}, bf16[8,352,3072]{2,1,0:T(8,128)(2,1)}, bf16[8,352,3072]{2,1,0:T(8,128)(2,1)}, bf16[8,352,3072]{2,1,0:T(8,128)(2...) custom-call(bf16[5632,3072]{1,0:T(8,128)(2,1)} %get-tuple-element.14, ...), custom_call_target="tpu_custom_call", output_to_operand_aliasing={{0}: (0, {})} | custom-call | flops 159450660864 | bytes 300000000 | tf_op jit(solution)/shard_map/reduce/pallas_call | solution.py:663
  444.1 19.8 %copy.14 = (bf16[352,3072]{1,0:T(8,128)(2,1)}, bf16[3072,1536]{1,0:T(8,128)(2,1)}, bf16[3072,1536]{1,0:T(8,128)(2,1)}, bf16[1536,3072]{1,0:T(8,128)(2,1)}) custom-call(bf16[352,3072]{1,0:T(8,128)(2,1)} %get-tuple-element.20.refs_0_, bf16[3072,1536]{1,0:T(8,128)(2,1)} %get-tuple-element.21.refs_1_, bf16[3072,1536]{1,0:T(8,128)(2,1)} %get-tuple-element.22.refs_2_, ...), custom_call_target="tpu_custom_call" | custom-call | flops 1000000 | bytes 61000000 | tf_op jit(solution)/shard_map/copy/pallas_call | solution.py:695

commit v3 on v2

--- a/solution.py
+++ b/solution.py
@@ -7,7 +7,6 @@
 
 R, D, F = 352, 3072, 1536
 H = R // 2
-RA = 264
 RING = 8
 NC = 2
 CH = F
@@ -56,6 +55,10 @@
     return 2 * o + other
 
 
+def home(zs):
+    return jnp.where(zs == 0, 1, jnp.where(zs == 3, 2, zs))
+
+
 def greet(y, z, c):
     bar = pltpu.get_barrier_semaphore()
 
@@ -82,7 +85,9 @@
     pltpu.make_async_copy(dst, dst, sem).wait()
 
 
-XPARTS = ((0, RA), (RA, R - RA))
+XPARTS = ((0, 176), (176, 88), (264, 88))
+PARTS = (0, 1, 2)
+CROSS = 2
 PIECE = 88
 BOTH = (0, 1)
 
@@ -162,17 +167,39 @@
         cols = pl.ds(j * CH, CH)
         return pltpu.make_async_copy(pv.at[:, cols], pf.at[s, :, cols], p_s.at[j])
 
-    ways = ((z < 3, (y * 4 + z + 1) * 2 + c, 0, z + 1), (z > 0, (y * 4 + z - 1) * 2 + c, 0, z - 1),
-            (z >= 0, ((1 - y) * 4 + z) * 2 + c, 1, z))
+    inner = home(z) == z
+    over = ((1 - y) * 4 + z) * 2 + c
+    ways = ((z < 3, (y * 4 + z + 1) * 2 + c, 0, z + 1), (z > 0, (y * 4 + z - 1) * 2 + c, 0, z - 1), (z >= 0, over, 1, z))
+    comes = (z > 0, z < 3, z >= 0)
+
+    def first_hop(w, part, there):
+        if w == 3:
+            return z >= 0
+        if w == 2:
+            return inner if part == CROSS else there[w]
+        return there[w] if part != 1 else z < 0
 
     def x_send(w, part):
         r0, n = XPARTS[part]
+        src = x.at[pl.ds(r0, n)]
+        if w == 3:
+            return remote(src, xf.at[xplace(z, 0, z, part, False)], x_t.at[w, part], x_r.at[w, part], mate)
         _, target, other, zt = ways[w]
-        return remote(x.at[pl.ds(r0, n)], xf.at[xplace(zt, other, z, part, True)], x_t.at[w, part], x_r.at[w, part], target)
-
-    def x_mate(part):
-        r0, n = XPARTS[part]
-        return remote(x.at[pl.ds(r0, n)], xf.at[xplace(z, 0, z, part, False)], x_t.at[3, part], x_r.at[3, part], mate)
+        return remote(src, xf.at[xplace(zt, other, z, part, True)], x_t.at[w, part], x_r.at[w, part], target)
+
+    zc = jnp.where(z == 1, 0, 3)
+    crossing = remote(xf.at[xplace(z, 0, zc, CROSS, True)], xf.at[xplace(z, 1, zc, CROSS, True)],
+                      x_t.at[4, CROSS], x_r.at[4, CROSS], over)
+
+    def x_here(w, part):
+        arrived(x_r.at[w, part], xf.at[pl.ds(0, XPARTS[part][1])])
+
+    def cross():
+        for w, zi in ((0, 1), (1, 2)):
+            @pl.when(z == zi)
+            def _():
+                x_here(w, CROSS)
+                crossing.start()
 
     weights[0].start()
     for cp in loads(0, 1, True):
@@ -207,12 +234,12 @@
                     ring_copy(p, s + 2, side, part).start()
                 mate_copy(p, s + 1, side, part).start()
 
-    def x_leaves(part):
-        for w in range(3):
-            @pl.when(ways[w][0])
-            def _():
-                x_send(w, part).start()
-        x_mate(part).start()
+    def x_leaves():
+        for part in reversed(PARTS):
+            for w in range(4):
+                @pl.when(first_hop(w, part, [way[0] for way in ways]))
+                def _():
+                    x_send(w, part).start()
 
     def step(s, carry):
         for cp in loads(s, 1):
@@ -255,6 +282,10 @@
             partial_dx(j, put_p)
             p_store(s, j).start()
         advance(s, 0)
+
+        @pl.when(s == RING - 1)
+        def _():
+            cross()
 
         for cp in loads(s, 0):
             cp.wait()
@@ -278,10 +309,10 @@
         @pl.when(s < RING - 1)
         def _():
             loads(s + 1, 1)[0].start()
-        for part in BOTH:
-            @pl.when(s == XSTEPS[part])
-            def _():
-                x_leaves(part)
+
+        @pl.when(s == XSTEP)
+        def _():
+            x_leaves()
         partial_dx(1, put_q)
         q_send(s, 1).start()
         return carry
@@ -293,19 +324,24 @@
     for j in range(NC):
         p_store(0, j).wait()
         q_send(0, j).wait_send()
-    comes = (z > 0, z < 3, z >= 0)
-    for part in BOTH:
-        n = XPARTS[part][1]
-        for w in range(3):
-            @pl.when(comes[w])
-            def _():
-                arrived(x_r.at[w, part], xf.at[pl.ds(0, n)])
-
-            @pl.when(ways[w][0])
+    for part in PARTS:
+        for w in range(4):
+            took = first_hop(w, part, comes)
+            if part == CROSS and w < 2:
+                took = took & (z != w + 1)
+
+            @pl.when(took)
+            def _():
+                x_here(w, part)
+
+            @pl.when(first_hop(w, part, [way[0] for way in ways]))
             def _():
                 x_send(w, part).wait_send()
-        arrived(x_r.at[3, part], xf.at[pl.ds(0, n)])
-        x_mate(part).wait_send()
+
+    @pl.when(inner)
+    def _():
+        x_here(4, CROSS)
+        crossing.wait_send()
 
     def drain(s, carry):
         for part in BOTH:
@@ -322,7 +358,7 @@
     lax.fori_loop(0, RING, drain, 0)
 
 
-XSTEPS = (5, 5)
+XSTEP = 5
 
 
 def back_call(x, dy, gate, up, wd, wg, wu):
@@ -343,7 +379,7 @@
             pltpu.VMEM((R, D), F32), pltpu.VMEM((NC, R, CH), BF),
             dma((3,)), dma((2, 5)), dma((2,)), dma((3,)), dma((NC,)),
             dma((RING, 2, 2)), dma((RING, 2, 2)), dma((RING, 2, 2)), dma((RING, 2, 2)),
-            dma((RING, NC)), dma((NC,)), dma((4, 2)), dma((4, 2)),
+            dma((RING, NC)), dma((NC,)), dma((5, 3)), dma((5, 3)),
         ],
         compiler_params=pltpu.CompilerParams(collective_id=0, has_side_effects=True, vmem_limit_bytes=66_000_000),
         cost_estimate=pl.CostEstimate(flops=3 * 2 * 16 * R * D * F, bytes_accessed=300_000_000, transcendentals=16 * R * F),
@@ -364,16 +400,18 @@
 GU = 2 * DOWN
 GU_OUT = 4
 ENDS = "".join((
-    "CJIDSZYTZYZZZyZYUZYZZzZYVZYZZEKmZYZZZLoZYZZFZpZYZZ",
-    "QZYuZYZZnZYRZYZZGMvZYZZZNkZYZZZHlZYZZZPiZYwZYZZjZY",
-    "xZYZOeZYsZYZZgZYtZYZZhZYqZYZZfZYcZYrZYZZZdZYaZYZbY",
+    "DMFN2ZYyZYZZ4ZEYuZYZZZPmZYZZ0GQZYiZYZZRoZYZZZOeZYZ",
+    "ZwZSIY3ZYZ5ZHYkZYZZZgZYZZsZJTYzZYZZZUpZYZZZXvZYZZ1",
+    "ZVLYnZYZxZKYjZYZZZlZYZZqZWYcYfYZZtZYhZYZZaZYrZYZZd",
+    "ZYZZZbY",
 ))
 INNER = "".join((
-    "AELBFKZZZZZJZZZZZZZZZGIZZZZNSZYZZZHTZYZZPMZyZYZZZz",
-    "ZYZUZYmZYZZVZOYZZZQZYoZYnZYqZYRZYpZYrZYsZYkZZZYtZY",
-    "lZYaZZYwZYiZYcZYxZYjZZZYuZYdZYZZvZYbZYgZYZeZYhZYfY",
+    "AGROCIPQZZZZZBHZZZZMZZZZJZZZZUSZZZZXNZZZ2ZLTYZZyZY",
+    "4ZKYZZmZYZVZZiZY0ZWYZZ3ZYuZYZZoZYsZYZkZYqZY5ZYeZYz",
+    "ZYcZY1ZZYaZYpZYtZYwZYrZYnZYZvZYjZYdZYxZYZlZYbZYgZY",
+    "fZYZZhY",
 ))
-LETTERS = "ZABCDEFGHIJKLMNOPabcdefghijklmnopqrstuvwxyzQRSTUVY"
+LETTERS = "ZABCDEFGHIJKLMNOPQRSTUVWXabcdefghijklmnopqrstuvwxyz012345Y"
 SUMS = LETTERS.index("a")
 ADD = LETTERS.index("Y")
 BASE = 64
@@ -405,26 +443,40 @@
     def real(k):
         return jnp.where(z < 2, k, 3 - k)
 
+    def hop_up(other, zs, part):
+        src = xf.at[xplace(z, other, zs, part, True)]
+        return remote(src, xf.at[xplace(z + 1, other, zs, part, True)], x_t.at[0, other * 4 + zs, part],
+                      x_r.at[other * 4 + zs, part], above)
+
+    def hop_down(other, zs, part):
+        src = xf.at[xplace(z, other, zs, part, True)]
+        return remote(src, xf.at[xplace(z - 1, other, zs, part, True)], x_t.at[1, other * 4 + zs, part],
+                      x_r.at[other * 4 + zs, part], below)
+
     def x_sends(other, zs, part):
         src = xf.at[xplace(z, other, zs, part, True)]
         n = other * 4 + zs
-        turn = (other == 1) & (zs == z)
+        if part == CROSS:
+            root = jnp.where(other == 0, zs, home(zs))
+            turn = (other == 1) & (root == z)
+            go_up, go_down = (root < z) | turn, (root > z) | turn
+        else:
+            go_up, go_down = (other == 0) & (zs < z), (other == 0) & (zs > z)
+        out = [(go_up & (z < 3), hop_up(other, zs, part)), (go_down & (z > 0), hop_down(other, zs, part)),
+               (z >= 0, remote(src, xf.at[xplace(z, other, zs, part, False)], xd_t.at[n, part], xd_r.at[n, part], mate))]
+        if part != CROSS:
+            out.append((other == 0, remote(src, xf.at[xplace(z, 1 - other, zs, part, True)], x_t.at[2, n, part],
+                                           x_r.at[(1 - other) * 4 + zs, part], across)))
+        return out
+
+    def pass_on(other, zs, part):
+        near = (other == 0) & ((zs - z) * (zs - z) == 1)
         if part == 0:
-            go_up, go_down, go_over = (other == 0) & (zs < z), (other == 0) & (zs > z), other == 0
+            first = near | ((other == 1) & (zs == z))
+        elif part == 1:
+            first = (other == 1) & (zs == z)
         else:
-            go_up, go_down, go_over = (zs < z) | turn, (zs > z) | turn, None
-        out = [(go_up & (z < 3), remote(src, xf.at[xplace(z + 1, other, zs, part, True)], x_t.at[0, n, part],
-                                        x_r.at[n, part], above)),
-               (go_down & (z > 0), remote(src, xf.at[xplace(z - 1, other, zs, part, True)], x_t.at[1, n, part],
-                                          x_r.at[n, part], below)),
-               (z >= 0, remote(src, xf.at[xplace(z, other, zs, part, False)], xd_t.at[n, part], xd_r.at[n, part], mate))]
-        if go_over is not None:
-            out.append((go_over, remote(src, xf.at[xplace(z, 1 - other, zs, part, True)], x_t.at[2, n, part],
-                                        x_r.at[(1 - other) * 4 + zs, part], across)))
-        return out
-
-    def pass_on(other, zs, part):
-        first = ((other == 0) & ((zs - z) * (zs - z) == 1)) | ((other == 1) & (zs == z))
+            first = near | ((other == 1) & (home(zs) == z))
 
         @pl.when(jnp.logical_not(first))
         def _():
@@ -434,10 +486,12 @@
             def _():
                 cp.start()
 
+    own_hops = ((z < 3, hop_up(0, z, 1)), (z > 0, hop_down(0, z, 1)))
+
     def slot_from_mate(sl, carry):
         o, other = sl // 2, lax.rem(sl, 2)
         k = jnp.where(end | (o > 1), o, 1 - o)
-        for part in BOTH:
+        for part in PARTS:
             arrived(xd_r.at[other * 4 + real(k), part], xf.at[pl.ds(0, XPARTS[part][1])])
         return carry
 
@@ -605,6 +659,10 @@
     for cp in down_loads(0, 0):
         cp.start()
     greet(y, z, c)
+    for cond, cp in own_hops:
+        @pl.when(cond)
+        def _():
+            cp.start()
     tables = packed(ENDS), packed(INNER)
 
     def item(i, carry):
@@ -620,10 +678,10 @@
         @pl.when(code == 0)
         def _():
             unit(u)
-        for part in BOTH:
-            @pl.when((code > 0) & (code < SUMS) & (lax.rem(code + 1, 2) == part))
-            def _():
-                pass_on((code - 1) // 8, real(lax.rem((code - 1) // 2, 4)), part)
+        for part in PARTS:
+            @pl.when((code > 0) & (code < SUMS) & (lax.rem(code + 2, 3) == part))
+            def _():
+                pass_on((code - 1) // 12, real(lax.rem((code - 1) // 3, 4)), part)
 
         @pl.when((code >= SUMS) & (code < ADD))
         def _():
@@ -645,13 +703,17 @@
 
         @pl.when((other == 1) | (zs != z))
         def _():
-            for part in BOTH:
+            for part in PARTS:
                 for cond, cp in x_sends(other, zs, part):
                     @pl.when(cond)
                     def _():
                         cp.wait_send()
         return carry
     lax.fori_loop(0, RING, drain, 0)
+    for cond, cp in own_hops:
+        @pl.when(cond)
+        def _():
+            cp.wait_send()
 
 
 def reduce_call(xf, h, dyf, dgu, pf, qb):
@@ -670,7 +732,7 @@
             pltpu.VMEM((D, 2 * F), F32), pltpu.VMEM((2, BLK, D), BF), pltpu.VMEM((2, BLK, 2 * F), BF),
             pltpu.VMEM((2, CAST, D), BF), pltpu.VMEM((PIECE, D), F32), pltpu.VMEM((4, PIECE, D), BF),
             pltpu.VMEM((SLOTS, PIECE, D), BF),
-            dma((RING, 2)), dma((3, RING, 2)), dma((RING, 2)), dma((RING, 2)),
+            dma((RING, 3)), dma((3, RING, 3)), dma((RING, 3)), dma((RING, 3)),
             dma((RING, 4)), dma((RING, 4)), dma((RING, 4)), dma((SLOTS,)), dma((2, 4)), dma((2, 2)), dma((5,)),
         ],
         compiler_params=pltpu.CompilerParams(collective_id=1, has_side_effects=True, vmem_limit_bytes=66_000_000),

time: 464 us -> 458 us (0.987)
  Pallas kernels: 463 us -> 457 us
    pallas_call x1, Pallas kernels: 216 us -> 204 us  [back_call(): pl.pallas_call(back_kernel, out_shape=outs, in_specs=[hbm] * 7, out_specs...]
    pallas_call x1, Pallas kernels: 228 us -> 233 us  [reduce_call(): pl.pallas_call(reduce_kernel, out_shape=outs, in_specs=[hbm] * 6, out_spe...]
where the time goes in v3:
time: 458 us
  Pallas kernels  457 us (100%)
    pallas_call x1, Pallas kernels, reduce_call(): pl.pallas_call(reduce_kernel, out_shape=outs, in_specs=[hbm] * 6, out_spe...  233 us
    pallas_call x1, Pallas kernels, back_call(): pl.pallas_call(back_kernel, out_shape=outs, in_specs=[hbm] * 7, out_specs...  204 us
    pallas_call x1, Pallas kernels, copy_call(): pl.pallas_call(copy_kernel, grid=(n,), out_shape=[jax.ShapeDtypeStruct(a....  19.8 us

profile of v3, /device:TPU:0, one launch (start us, length us, event | category | flops | bytes accessed | tf_op | source)
XLA Modules:
  0.0 457.9 jit_solution(336697844007015325)
XLA Ops:
  0.6 204.1 %back.1 = (bf16[5632,1536]{1,0:T(8,128)(2,1)}, bf16[5632,3072]{1,0:T(8,128)(2,1)}, bf16[5632,3072]{1,0:T(8,128)(2,1)}, f32[8,352,3072]{2,1,0:T(8,128)}, bf16[8,3...) custom-call(bf16[352,3072]{1,0:T(8,128)(2,1)} %x.1, bf16[352,3072]{1,0:T(8,128)(2,1)} %dy.1, bf16[5632,1536]{1,0:T(8,128)(2,1)} %gate.1, ...), custom_call_target="tpu_custom_call" | custom-call | flops 159450660864 | bytes 300000000 | tf_op jit(solution)/shard_map/back/pallas_call | solution.py:370
  204.7 233.4 %reduce.1 = (bf16[5632,3072]{1,0:T(8,128)(2,1)}, bf16[8,352,3072]{2,1,0:T(8,128)(2,1)}, bf16[8,352,3072]{2,1,0:T(8,128)(2,1)}, bf16[8,352,3072]{2,1,0:T(8,128)(2...) custom-call(bf16[5632,3072]{1,0:T(8,128)(2,1)} %get-tuple-element.14, ...), custom_call_target="tpu_custom_call", output_to_operand_aliasing={{0}: (0, {})} | custom-call | flops 159450660864 | bytes 300000000 | tf_op jit(solution)/shard_map/reduce/pallas_call | solution.py:725
  438.1 19.8 %copy.14 = (bf16[352,3072]{1,0:T(8,128)(2,1)}, bf16[3072,1536]{1,0:T(8,128)(2,1)}, bf16[3072,1536]{1,0:T(8,128)(2,1)}, bf16[1536,3072]{1,0:T(8,128)(2,1)}) custom-call(bf16[352,3072]{1,0:T(8,128)(2,1)} %get-tuple-element.20.refs_0_, bf16[3072,1536]{1,0:T(8,128)(2,1)} %get-tuple-element.21.refs_1_, bf16[3072,1536]{1,0:T(8,128)(2,1)} %get-tuple-element.22.refs_2_, ...), custom_call_target="tpu_custom_call" | custom-call | flops 1000000 | bytes 61000000 | tf_op jit(solution)/shard_map/copy/pallas_call | solution.py:757

commit v4 on v3

--- a/solution.py
+++ b/solution.py
@@ -28,6 +28,9 @@
 
 
 MESH = pl.DeviceIdType.MESH
+FLOPS, BYTES = 6 * 16 * R * D * F, 300_000_000
+TOKENS = 16 * R
+VMEM = 66_000_000
 
 
 def place():
@@ -36,8 +39,12 @@
     return y, z, c, jnp.where(y == 0, z, 7 - z)
 
 
+def chip(y, z, core):
+    return (y * 4 + z) * 2 + core
+
+
 def dev(p, core):
-    return (p // 4 * 4 + jnp.where(p < 4, p, 7 - p)) * 2 + core
+    return chip(p // 4, jnp.where(p < 4, p, 7 - p), core)
 
 
 def start(pos, s, side, core):
@@ -64,16 +71,16 @@
 
     def hello(d):
         pl.semaphore_signal(bar, inc=1, device_id={"tp": d}, device_id_type=MESH)
-    hello((y * 4 + z) * 2 + 1 - c)
-    hello(((1 - y) * 4 + z) * 2 + c)
+    hello(chip(y, z, 1 - c))
+    hello(chip(1 - y, z, c))
 
     @pl.when(z < 3)
     def _():
-        hello((y * 4 + z + 1) * 2 + c)
+        hello(chip(y, z + 1, c))
 
     @pl.when(z > 0)
     def _():
-        hello((y * 4 + z - 1) * 2 + c)
+        hello(chip(y, z - 1, c))
     pl.semaphore_wait(bar, 2 + jnp.where(z < 3, 1, 0) + jnp.where(z > 0, 1, 0))
 
 
@@ -168,8 +175,8 @@
         return pltpu.make_async_copy(pv.at[:, cols], pf.at[s, :, cols], p_s.at[j])
 
     inner = home(z) == z
-    over = ((1 - y) * 4 + z) * 2 + c
-    ways = ((z < 3, (y * 4 + z + 1) * 2 + c, 0, z + 1), (z > 0, (y * 4 + z - 1) * 2 + c, 0, z - 1), (z >= 0, over, 1, z))
+    over = chip(1 - y, z, c)
+    ways = ((z < 3, chip(y, z + 1, c), 0, z + 1), (z > 0, chip(y, z - 1, c), 0, z - 1), (z >= 0, over, 1, z))
     comes = (z > 0, z < 3, z >= 0)
 
     def first_hop(w, part, there):
@@ -364,8 +371,8 @@
 def back_call(x, dy, gate, up, wd, wg, wu):
     sd = jax.ShapeDtypeStruct
     hbm = pl.BlockSpec(memory_space=pl.ANY)
-    outs = [sd((16 * R, F), BF), sd((16 * R, D), BF), sd((16 * R, 2 * F), BF), sd((RING, R, D), F32),
-            sd((RING, R, D), BF), sd((16 * R, D), BF)]
+    outs = [sd((TOKENS, F), BF), sd((TOKENS, D), BF), sd((TOKENS, 2 * F), BF), sd((RING, R, D), F32),
+            sd((RING, R, D), BF), sd((TOKENS, D), BF)]
     dma = pltpu.SemaphoreType.DMA
     return pl.pallas_call(
         back_kernel,
@@ -378,11 +385,11 @@
             pltpu.VMEM((R, 2 * F), BF), pltpu.VMEM((R, F), BF),
             pltpu.VMEM((R, D), F32), pltpu.VMEM((NC, R, CH), BF),
             dma((3,)), dma((2, 5)), dma((2,)), dma((3,)), dma((NC,)),
-            dma((RING, 2, 2)), dma((RING, 2, 2)), dma((RING, 2, 2)), dma((RING, 2, 2)),
+            *[dma((RING, 2, 2))] * 4,
             dma((RING, NC)), dma((NC,)), dma((5, 3)), dma((5, 3)),
         ],
-        compiler_params=pltpu.CompilerParams(collective_id=0, has_side_effects=True, vmem_limit_bytes=66_000_000),
-        cost_estimate=pl.CostEstimate(flops=3 * 2 * 16 * R * D * F, bytes_accessed=300_000_000, transcendentals=16 * R * F),
+        compiler_params=pltpu.CompilerParams(collective_id=0, has_side_effects=True, vmem_limit_bytes=VMEM),
+        cost_estimate=pl.CostEstimate(flops=FLOPS, bytes_accessed=BYTES, transcendentals=TOKENS * F),
         name="back",
     )(x, dy, gate, up, wd, wg, wu)
 
@@ -437,8 +444,7 @@
                   x_r, x_t, xd_r, xd_t, lo_r, hi_r, iy_r, ob_s, ld_s, st_s, in_s):
     y, z, c, pos = place()
     end = mirrored(z) == 0
-    above, below, across, mate = ((y * 4 + z + 1) * 2 + c, (y * 4 + z - 1) * 2 + c,
-                                  ((1 - y) * 4 + z) * 2 + c, (y * 4 + z) * 2 + 1 - c)
+    above, below, across, mate = chip(y, z + 1, c), chip(y, z - 1, c), chip(1 - y, z, c), chip(y, z, 1 - c)
 
     def real(k):
         return jnp.where(z < 2, k, 3 - k)
@@ -720,7 +726,7 @@
     sd = jax.ShapeDtypeStruct
     hbm = pl.BlockSpec(memory_space=pl.ANY)
     land = sd((RING, R, D), BF)
-    outs = [sd((16 * R, D), BF), land, land, land, sd((R, D), BF), sd((D, F), BF), sd((D, F), BF), sd((F, D), BF)]
+    outs = [sd((TOKENS, D), BF), land, land, land, sd((R, D), BF), sd((D, F), BF), sd((D, F), BF), sd((F, D), BF)]
     dma = pltpu.SemaphoreType.DMA
     return pl.pallas_call(
         reduce_kernel,
@@ -733,10 +739,10 @@
             pltpu.VMEM((2, CAST, D), BF), pltpu.VMEM((PIECE, D), F32), pltpu.VMEM((4, PIECE, D), BF),
             pltpu.VMEM((SLOTS, PIECE, D), BF),
             dma((RING, 3)), dma((3, RING, 3)), dma((RING, 3)), dma((RING, 3)),
-            dma((RING, 4)), dma((RING, 4)), dma((RING, 4)), dma((SLOTS,)), dma((2, 4)), dma((2, 2)), dma((5,)),
+            *[dma((RING, 4))] * 3, dma((SLOTS,)), dma((2, 4)), dma((2, 2)), dma((5,)),
         ],
-        compiler_params=pltpu.CompilerParams(collective_id=1, has_side_effects=True, vmem_limit_bytes=66_000_000),
-        cost_estimate=pl.CostEstimate(flops=3 * 2 * 16 * R * D * F, bytes_accessed=300_000_000, transcendentals=0),
+        compiler_params=pltpu.CompilerParams(collective_id=1, has_side_effects=True, vmem_limit_bytes=VMEM),
+        cost_estimate=pl.CostEstimate(flops=FLOPS, bytes_accessed=BYTES, transcendentals=0),
         name="reduce",
     )(xf, h, dyf, dgu, pf, qb)
 
@@ -760,7 +766,7 @@
         out_shape=[jax.ShapeDtypeStruct(a.shape, a.dtype) for a in (dx, og, ou, od)],
         in_specs=specs,
         out_specs=specs,
-        compiler_params=pltpu.CompilerParams(dimension_semantics=("arbitrary",), vmem_limit_bytes=66_000_000),
+        compiler_params=pltpu.CompilerParams(dimension_semantics=("arbitrary",), vmem_limit_bytes=VMEM),
         cost_estimate=pl.CostEstimate(flops=1_000_000, bytes_accessed=61_000_000, transcendentals=0),
         name="copy",
     )(dx, og, ou, od)

time: 458 us -> 458 us (level)
  no operation moved by 1% of the time
where the time goes in v4:
time: 458 us
  Pallas kernels  457 us (100%)
    pallas_call x1, Pallas kernels, reduce_call(): pl.pallas_call(reduce_kernel, out_shape=outs, in_specs=[hbm] * 6, out_spe...  233 us
    pallas_call x1, Pallas kernels, back_call(): pl.pallas_call(back_kernel, out_shape=outs, in_specs=[hbm] * 7, out_specs...  204 us
    pallas_call x1, Pallas kernels, copy_call(): pl.pallas_call(copy_kernel, grid=(n,), out_shape=[jax.ShapeDtypeStruct(a....  19.8 us

profile of v4, /device:TPU:0, one launch (start us, length us, event | category | flops | bytes accessed | tf_op | source)
XLA Modules:
  0.0 457.7 jit_solution(12694424441427158156)
XLA Ops:
  0.6 204.1 %back.1 = (bf16[5632,1536]{1,0:T(8,128)(2,1)}, bf16[5632,3072]{1,0:T(8,128)(2,1)}, bf16[5632,3072]{1,0:T(8,128)(2,1)}, f32[8,352,3072]{2,1,0:T(8,128)}, bf16[8,3...) custom-call(bf16[352,3072]{1,0:T(8,128)(2,1)} %x.1, bf16[352,3072]{1,0:T(8,128)(2,1)} %dy.1, bf16[5632,1536]{1,0:T(8,128)(2,1)} %gate.1, ...), custom_call_target="tpu_custom_call" | custom-call | flops 159450660864 | bytes 300000000 | tf_op jit(solution)/shard_map/back/pallas_call | solution.py:377
  204.7 233.2 %reduce.1 = (bf16[5632,3072]{1,0:T(8,128)(2,1)}, bf16[8,352,3072]{2,1,0:T(8,128)(2,1)}, bf16[8,352,3072]{2,1,0:T(8,128)(2,1)}, bf16[8,352,3072]{2,1,0:T(8,128)(2...) custom-call(bf16[5632,3072]{1,0:T(8,128)(2,1)} %get-tuple-element.14, ...), custom_call_target="tpu_custom_call", output_to_operand_aliasing={{0}: (0, {})} | custom-call | flops 159450660864 | bytes 300000000 | tf_op jit(solution)/shard_map/reduce/pallas_call | solution.py:731
  437.9 19.8 %copy.14 = (bf16[352,3072]{1,0:T(8,128)(2,1)}, bf16[3072,1536]{1,0:T(8,128)(2,1)}, bf16[3072,1536]{1,0:T(8,128)(2,1)}, bf16[1536,3072]{1,0:T(8,128)(2,1)}) custom-call(bf16[352,3072]{1,0:T(8,128)(2,1)} %get-tuple-element.20.refs_0_, bf16[3072,1536]{1,0:T(8,128)(2,1)} %get-tuple-element.21.refs_1_, bf16[3072,1536]{1,0:T(8,128)(2,1)} %get-tuple-element.22.refs_2_, ...), custom_call_target="tpu_custom_call" | custom-call | flops 1000000 | bytes 61000000 | tf_op jit(solution)/shard_map/copy/pallas_call | solution.py:763
